TPU v7x, 8 devices: a whole 2x2x1 slice. The times are simulated.
8 devices in a mesh: pod: 1 (over z), dp: 2 (over y), ep: 4 (over x, core).
Axes of the slice: x: 2, y: 2, z: 1, core: 2. Of those that a mesh axis runs over, the one named last changes fastest.
Arguments:
- x_start: bfloat16 [8192, 1024], P(('pod', 'dp', 'ep'))
- route_a: int32 [8192, 2], P(('pod', 'dp', 'ep'))
- route_b: int32 [8192, 2], P(('pod', 'dp', 'ep'))
- gate_a: float32 [8192, 2], P(('pod', 'dp', 'ep'))
- gate_b: float32 [8192, 2], P(('pod', 'dp', 'ep'))
- grad_out: bfloat16 [8192, 1024], P(('pod', 'dp', 'ep'))
- w1_a: bfloat16 [16, 1024, 1536], P('ep')
- w3_a: bfloat16 [16, 1024, 1536], P('ep')
- w2_a: bfloat16 [16, 1536, 1024], P('ep')
- w1_b: bfloat16 [16, 1024, 1536], P('ep')
- w3_b: bfloat16 [16, 1024, 1536], P('ep')
- w2_b: bfloat16 [16, 1536, 1024], P('ep')
Outputs:
- output 1: bfloat16 [8192, 1024], P(('pod', 'dp', 'ep'))
- output 2: bfloat16 [8192, 1024], P(('pod', 'dp', 'ep'))
- output 3: float32 [16, 1024, 1536], P(('pod', 'ep'), 'dp')
- output 4: float32 [16, 1024, 1536], P(('pod', 'ep'), 'dp')
- output 5: float32 [16, 1536, 1024], P(('pod', 'ep'), 'dp')
- output 6: float32 [16, 1024, 1536], P(('pod', 'ep'), 'dp')
- output 7: float32 [16, 1024, 1536], P(('pod', 'ep'), 'dp')
- output 8: float32 [16, 1536, 1024], P(('pod', 'ep'), 'dp')
- output 9: float32 [8192, 2], P(('pod', 'dp', 'ep'))
- output 10: float32 [8192, 2], P(('pod', 'dp', 'ep'))
All inputs are finite; a program needn't handle non-finite values.
Results may differ from a plain program's by a relative error of at most 0.0078204.
Values are sent between devices in bfloat16 or wider.
A program may use at most 1 GiB of HBM per device.

v0:
```python
import jax
import jax.numpy as jnp
from jax import lax
from jax.sharding import PartitionSpec as P


def route_rows(expert_ids, n_experts, capacity):
    n_tokens, top_k = expert_ids.shape
    flat_ids = expert_ids.reshape(-1)
    onehot = (flat_ids[:, None] == jnp.arange(n_experts, dtype=jnp.int32)[None, :]).astype(jnp.int32)
    earlier = jnp.cumsum(onehot, axis=0) - onehot
    slot_idx = jnp.sum(earlier * onehot, axis=1)
    pair_row = flat_ids * capacity + slot_idx
    pair_tok = jnp.arange(n_tokens * top_k, dtype=jnp.int32) // top_k
    row_tok = jnp.zeros((n_experts * capacity,), jnp.int32).at[pair_row].set(pair_tok)
    row_used = jnp.zeros((n_experts * capacity,), jnp.bfloat16).at[pair_row].set(1.0)
    return pair_row, row_tok, row_used


def take_rows(values, row_tok, row_used):
    return jnp.take(values, row_tok, axis=0) * row_used[:, None]


def place_gates(gate_vals, pair_row, n_rows):
    return jnp.zeros((n_rows,), jnp.float32).at[pair_row].set(gate_vals.reshape(-1))


def mix_back(x_in, out_rows, pair_row, gate_vals):
    n_tokens, top_k = gate_vals.shape
    pair_out = jnp.take(out_rows, pair_row, axis=0).reshape(n_tokens, top_k, -1)
    mixed_sum = jnp.sum(gate_vals[:, :, None] * pair_out, axis=1)
    return (x_in.astype(jnp.float32) + mixed_sum).astype(jnp.bfloat16)


def add_back(grad_in, du_rows, pair_row, gate_grad_rows, top_k):
    n_tokens = grad_in.shape[0]
    pair_grad = jnp.take(du_rows, pair_row, axis=0).reshape(n_tokens, top_k, -1)
    grad_x = (grad_in.astype(jnp.float32) + jnp.sum(pair_grad, axis=1, dtype=jnp.float32)).astype(jnp.bfloat16)
    return grad_x, jnp.take(gate_grad_rows, pair_row, axis=0).reshape(n_tokens, top_k)


def expert_forward(recv_rows, w_up1, w_up3, w_down):
    pre_one = jnp.einsum('secd,edf->escf', recv_rows, w_up1, preferred_element_type=jnp.float32)
    pre_three = jnp.einsum('secd,edf->escf', recv_rows, w_up3, preferred_element_type=jnp.float32)
    hidden = (jax.nn.silu(pre_one) * pre_three).astype(jnp.bfloat16)
    return jnp.einsum('escf,efd->secd', hidden, w_down, preferred_element_type=jnp.float32).astype(jnp.bfloat16)


def expert_backward(recv_rows, recv_dy, recv_gate, w_up1, w_up3, w_down):
    pre_one = jnp.einsum('secd,edf->escf', recv_rows, w_up1, preferred_element_type=jnp.float32)
    pre_three = jnp.einsum('secd,edf->escf', recv_rows, w_up3, preferred_element_type=jnp.float32)
    sig_one = jax.nn.sigmoid(pre_one)
    act_one = pre_one * sig_one
    hidden = (act_one * pre_three).astype(jnp.bfloat16)
    back_proj = jnp.einsum('secd,efd->escf', recv_dy, w_down, preferred_element_type=jnp.float32)
    gate_grad = jnp.sum(back_proj * hidden, axis=-1)
    gate_esc = jnp.transpose(recv_gate, (1, 0, 2))
    scaled_dy = (recv_gate[..., None] * recv_dy).astype(jnp.bfloat16)
    dw_down = jnp.einsum('escf,secd->efd', hidden, scaled_dy, preferred_element_type=jnp.float32)
    d_hidden = gate_esc[..., None] * back_proj
    d_pre_one = (d_hidden * pre_three * sig_one * (1.0 + pre_one * (1.0 - sig_one))).astype(jnp.bfloat16)
    d_pre_three = (d_hidden * act_one).astype(jnp.bfloat16)
    dw_up1 = jnp.einsum('secd,escf->edf', recv_rows, d_pre_one, preferred_element_type=jnp.float32)
    dw_up3 = jnp.einsum('secd,escf->edf', recv_rows, d_pre_three, preferred_element_type=jnp.float32)
    grad_rows = (jnp.einsum('escf,edf->secd', d_pre_one, w_up1, preferred_element_type=jnp.float32)
                 + jnp.einsum('escf,edf->secd', d_pre_three, w_up3, preferred_element_type=jnp.float32)).astype(jnp.bfloat16)
    return grad_rows, jnp.transpose(gate_grad, (1, 0, 2)), dw_up1, dw_up3, dw_down


def solution(mesh):
    n_ep = mesh.shape['ep']
    tok_spec = P(('pod', 'dp', 'ep'), None)
    weight_spec = P('ep', None, None)
    grad_spec = P(('pod', 'ep'), 'dp', None)

    def local_step(x_start, route_a, route_b, gate_a, gate_b, grad_out, w1_a, w3_a, w2_a, w1_b, w3_b, w2_b):
        n_tokens = x_start.shape[0]
        top_k = route_a.shape[1]
        n_local = w1_a.shape[0]
        n_experts = n_local * n_ep
        capacity = 3 * n_tokens * top_k // (2 * n_experts)
        n_rows = n_experts * capacity

        def exchange(send_rows):
            shaped = send_rows.reshape((n_ep, n_local, capacity) + send_rows.shape[1:])
            return lax.all_to_all(shaped, 'ep', 0, 0)

        def give_back(expert_rows):
            returned = lax.all_to_all(expert_rows, 'ep', 0, 0)
            return returned.reshape((n_rows,) + expert_rows.shape[3:])

        def layer_backward(recv_rows, grad_in, route_plan, gate_vals, w_up1, w_up3, w_down):
            pair_row, row_tok, row_used = route_plan
            recv_dy = exchange(take_rows(grad_in, row_tok, row_used))
            recv_gate = exchange(place_gates(gate_vals, pair_row, n_rows))
            grad_rows, gate_grad, dw_up1, dw_up3, dw_down = expert_backward(recv_rows, recv_dy, recv_gate, w_up1, w_up3, w_down)
            grad_x, gate_out = add_back(grad_in, give_back(grad_rows), pair_row, give_back(gate_grad), top_k)
            dw_parts = [lax.psum_scatter(grad_part, 'dp', scatter_dimension=1, tiled=True) for grad_part in (dw_up1, dw_up3, dw_down)]
            return grad_x, gate_out, dw_parts[0], dw_parts[1], dw_parts[2]

        plan_a = route_rows(route_a, n_experts, capacity)
        plan_b = route_rows(route_b, n_experts, capacity)
        recv_a = exchange(take_rows(x_start, plan_a[1], plan_a[2]))
        x_mid = mix_back(x_start, give_back(expert_forward(recv_a, w1_a, w3_a, w2_a)), plan_a[0], gate_a)
        recv_b = exchange(take_rows(x_mid, plan_b[1], plan_b[2]))
        x_final = mix_back(x_mid, give_back(expert_forward(recv_b, w1_b, w3_b, w2_b)), plan_b[0], gate_b)
        x_kept, recv_b_kept, grad_kept = lax.optimization_barrier((x_start, recv_b, grad_out))
        grad_mid, dgate_b, dw1_b, dw3_b, dw2_b = layer_backward(recv_b_kept, grad_kept, plan_b, gate_b, w1_b, w3_b, w2_b)
        recv_a_again = exchange(take_rows(x_kept, plan_a[1], plan_a[2]))
        grad_x, dgate_a, dw1_a, dw3_a, dw2_a = layer_backward(recv_a_again, grad_mid, plan_a, gate_a, w1_a, w3_a, w2_a)
        return (x_final, grad_x, dw1_a, dw3_a, dw2_a, dw1_b, dw3_b, dw2_b, dgate_a, dgate_b)

    return jax.shard_map(local_step, mesh=mesh,
                         in_specs=(tok_spec,) * 6 + (weight_spec,) * 6,
                         out_specs=(tok_spec, tok_spec) + (grad_spec,) * 6 + (tok_spec, tok_spec),
                         check_vma=False)
```

profile of v0, /device:TPU:0, one launch (start us, length us, event | category | flops | bytes accessed | tf_op | source)
XLA Modules:
  0.0 2237.6 jit_solution(1624951278598938925)
XLA Ops:
  23.6 14.6 scatter_custom_fusion.1
  38.2 13.9 gather_fusion
  56.1 75.2 %all_to_all.65 = bf16[4,4,192,1024]{3,2,1,0:T(8,128)(2,1)S(1)} all-to-all(bf16[4,4,192,1024]{3,2,1,0:T(8,128)(2,1)S(1)} %bitcast.163), channel_id=1, replica_groups=mesh['pod'=1,'dp'=2,'ep'=4] {'ep'}, dimensions={0} | all-to-all | bytes 12582912 | tf_op jit(solution)/shard_map/all_to_all | solution.py:86
  134.0 16.5 fusion.11
  150.5 27.4 %convert_bitcast_fusion.1 = bf16[4,4,192,1024]{3,2,0,1:T(8,128)(2,1)} fusion(bf16[4,1536,1024]{2,1,0:T(8,128)(2,1)} %param.26, f32[4,4,192,1536]{3,2,1,0:T(8,128)} %fusion.11, bf16[4,1024,1536]{2,1,0:T(8,128)(2,1)} %param.24, bf16[4,4,192,1024]{3,2,1,0:T(8,128)(2,1)} %copy-done.6), kind=kOutput, calls=%fused_computation.89 | convolution fusion | flops 19358810112 | bytes 56623104 | tf_op jit(solution)/shard_map/escf,efd->secd/dot_general | solution.py:46
  196.8 14.6 scatter_custom_fusion.3
  220.3 40.1 %all-to-all-done.1 = bf16[4,4,192,1024]{3,2,1,0:T(8,128)(2,1)} async-done(((bf16[4,4,192,1024]{3,2,1,0:T(8,128)(2,1)}), bf16[4,4,192,1024]{3,2,1,0:T(8,128)(2,1)}, u32[]{:S(2)}, u32[]{:S(2)}) %all-to-all-start.1) | async-done | bytes 6291488 | tf_op jit(solution)/shard_map/all_to_all | solution.py:89
  260.4 14.5 gather_fusion.1
  290.8 11.9 multiply_reduce_fusion.3
  304.9 17.7 gather_fusion.2
  344.1 61.1 %all-to-all-done.2 = bf16[4,4,192,1024]{3,2,1,0:T(8,128)(2,1)} async-done(((bf16[4,4,192,1024]{3,2,1,0:T(8,128)(2,1)}), bf16[4,4,192,1024]{3,2,1,0:T(8,128)(2,1)}, u32[]{:S(2)}, u32[]{:S(2)}) %all-to-all-start.2) | async-done | bytes 6291488 | tf_op jit(solution)/shard_map/all_to_all | solution.py:86
  408.4 13.9 gather_fusion.4
  434.6 19.3 fusion.19
  453.9 19.2 fusion.24
  473.1 31.6 %all-to-all-done.5 = bf16[4,4,192,1024]{3,2,1,0:T(8,128)(2,1)} async-done(((bf16[4,4,192,1024]{3,2,1,0:T(8,128)(2,1)}), bf16[4,4,192,1024]{3,2,1,0:T(8,128)(2,1)}, u32[]{:S(2)}, u32[]{:S(2)}) %all-to-all-start.5) | async-done | bytes 6291488 | tf_op jit(solution)/shard_map/all_to_all | solution.py:86
  504.7 32.8 %multiply_reduce_fusion = (f32[4,4,192]{2,1,0:T(4,128)}, bf16[4,4,192,1536]{3,2,1,0:T(8,128)(2,1)}, bf16[4,4,192,1536]{3,2,1,0:T(8,128)(2,1)}, bf16[4,4,192,1536]{3,2,1,0:T(8,128)(2,1)}) fusion(f32[4,4,192,1536]{3,2,1,0:T(8,128)} %fusion.24, f32[4,4,192,1536]{3,2,1,0:T(8,128)} %fusion.19, f32[4,4,192]{2,1,0:T(4,128)S(1)} %copy.100, ...), kind=kOutput, calls=%fused_computation.17 | convolution fusion | flops 9753326592 | bytes 84959232 | tf_op jit(solution)/shard_map/secd,efd->escf/dot_general | solution.py:55
  537.6 19.5 convolution_bitcast_fusion.2
  557.1 19.3 convolution_bitcast_fusion.3
  576.6 19.7 convolution_bitcast_fusion
  596.3 19.3 fusion.26
  615.6 27.6 %convert_bitcast_fusion = bf16[4,4,192,1024]{3,2,0,1:T(8,128)(2,1)} fusion(bf16[4,1536,1024]{2,1,0:T(8,128)(2,1)} %param.29, f32[4,4,192,1536]{3,2,1,0:T(8,128)} %fusion.26, bf16[4,1024,1536]{2,1,0:T(8,128)(2,1)} %param.27, bf16[4,4,192,1024]{3,2,1,0:T(8,128)(2,1)} %all-to-all-done.2), kind=kOutput, calls=%fused_computation.88 | convolution fusion | flops 19358810112 | bytes 56623104 | tf_op jit(solution)/shard_map/escf,efd->secd/dot_general | solution.py:46
  655.6 18.4 fusion.17
  674.1 51.3 %all-to-all-done.3 = bf16[4,4,192,1024]{3,2,1,0:T(8,128)(2,1)} async-done(((bf16[4,4,192,1024]{3,2,1,0:T(8,128)(2,1)}), bf16[4,4,192,1024]{3,2,1,0:T(8,128)(2,1)}, u32[]{:S(2)}, u32[]{:S(2)}) %all-to-all-start.3) | async-done | bytes 6291488 | tf_op jit(solution)/shard_map/all_to_all | solution.py:89
  728.6 18.9 fusion.36
  769.0 13.9 gather_fusion.7
  782.9 14.6 gather_fusion.3
  809.9 20.2 all-to-all-done.6
  833.4 14.5 gather_fusion.5
  867.2 13.0 reduce_sum.82
  883.8 13.9 gather_fusion.6
  908.2 77.0 %all_to_all.66 = bf16[4,4,192,1024]{3,2,1,0:T(8,128)(2,1)} all-to-all(bf16[4,4,192,1024]{3,2,1,0:T(8,128)(2,1)} %bitcast.165), channel_id=1, replica_groups=mesh['pod'=1,'dp'=2,'ep'=4] {'ep'}, dimensions={0} | all-to-all | bytes 12582912 | tf_op jit(solution)/shard_map/all_to_all | solution.py:86
  990.6 19.8 fusion.4
  1010.4 16.5 fusion.9
  1026.9 34.0 %all-to-all-done.8 = bf16[4,4,192,1024]{3,2,1,0:T(8,128)(2,1)} async-done(((bf16[4,4,192,1024]{3,2,1,0:T(8,128)(2,1)}), bf16[4,4,192,1024]{3,2,1,0:T(8,128)(2,1)}, u32[]{:S(2)}, u32[]{:S(2)}) %all-to-all-start.8) | async-done | bytes 6291488 | tf_op jit(solution)/shard_map/all_to_all | solution.py:86
  1060.9 32.2 %multiply_reduce_fusion.1 = (f32[4,4,192]{2,1,0:T(4,128)S(1)}, bf16[4,4,192,1536]{3,2,1,0:T(8,128)(2,1)}, bf16[4,4,192,1536]{3,2,1,0:T(8,128)(2,1)}, bf16[4,4,192,1536]{3,2,1,0:T(8,128)(2,1)}) fusion(f32[4,4,192,1536]{3,2,1,0:T(8,128)} %fusion.9, f32[4,4,192,1536]{3,2,1,0:T(8,128)} %fusion.4, f32[4,4,192]{2,1,0:T(4,128)S(1)} %copy.106, ...), kind=kOutput, calls=%fused_computation.18 | convolution fusion | flops 9753326592 | bytes 84959232 | tf_op jit(solution)/shard_map/secd,efd->escf/dot_general | solution.py:55
  1093.1 19.6 convolution_bitcast_fusion.4
  1112.8 19.4 convolution_bitcast_fusion.5
  1132.3 19.6 convolution_bitcast_fusion.1
  1155.7 18.3 fusion.2
  1174.0 18.9 fusion.37
  1217.0 12.0 multiply_reduce_fusion.2
  1244.3 31.1 %all-to-all-done.10 = bf16[4,4,192,1024]{3,2,1,0:T(8,128)(2,1)} async-done(((bf16[4,4,192,1024]{3,2,1,0:T(8,128)(2,1)}), bf16[4,4,192,1024]{3,2,1,0:T(8,128)(2,1)}, u32[]{:S(2)}, u32[]{:S(2)}) %all-to-all-start.10) | async-done | bytes 6291488 | tf_op jit(solution)/shard_map/all_to_all | solution.py:89
  1275.4 14.6 gather_fusion.8
  1305.7 13.0 reduce_sum.83
  1323.0 69.6 %reduce-scatter.17.cloned.1.call-done = f32[4,768,1024]{2,1,0:T(8,128)} async-done(((f32[4,1536,1024]{2,1,0:T(8,128)}), f32[4,768,1024]{2,1,0:T(8,128)}) %reduce-scatter.17.cloned.1.call-update) | async-done | bytes 12582928 | tf_op jit(solution)/shard_map/reduce_scatter | solution.py:98
  1392.7 279.2 %reduce-scatter.9.cloned.1.call-done = f32[4,512,1536]{2,1,0:T(8,128)} async-done(((f32[4,1024,1536]{2,1,0:T(8,128)}), f32[4,512,1536]{2,1,0:T(8,128)}) %reduce-scatter.9.cloned.1.call-update) | async-done | bytes 12582928 | tf_op jit(solution)/shard_map/reduce_scatter | solution.py:98
  1671.9 279.2 %reduce-scatter.7.cloned.1.call-done = f32[4,512,1536]{2,1,0:T(8,128)} async-done(((f32[4,1024,1536]{2,1,0:T(8,128)}), f32[4,512,1536]{2,1,0:T(8,128)}) %reduce-scatter.7.cloned.1.call-update) | async-done | bytes 12582928 | tf_op jit(solution)/shard_map/reduce_scatter | solution.py:98
  1951.1 279.2 %reduce-scatter.11.cloned.1.call-done = f32[4,768,1024]{2,1,0:T(8,128)} async-done(((f32[4,1536,1024]{2,1,0:T(8,128)}), f32[4,768,1024]{2,1,0:T(8,128)}) %reduce-scatter.11.cloned.1.call-update) | async-done | bytes 12582928 | tf_op jit(solution)/shard_map/reduce_scatter | solution.py:98
  (174 shorter events, 260.4 us)
Async XLA Ops:
  7.2 31.0 %copy-start = (bf16[1024,1024]{1,0:T(8,128)(2,1)S(1)}, bf16[1024,1024]{1,0:T(8,128)(2,1)}, u32[]{:S(2)}) copy-start(bf16[1024,1024]{1,0:T(8,128)(2,1)} %param.18) | copy-start | bytes 6291460
  15.4 36.6 %copy-start.30 = (s32[2048,1]{0,1:T(1,128)}, s32[2048,1]{0,1:T(1,128)S(1)}, u32[]{:S(2)}) copy-start(s32[2048,1]{0,1:T(1,128)S(1)} %compare_select_fusion.1) | copy-start | bytes 24580
  23.5 28.5 %copy-start.25 = (pred[3072]{0:T(1024)(128)(4,1)}, pred[3072]{0:T(1024)(128)(4,1)S(1)}, u32[]{:S(2)}) copy-start(pred[3072]{0:T(1024)(128)(4,1)S(1)} %compare_and_fusion.1) | copy-start | bytes 9220
  23.6 28.5 %copy-start.11 = (s32[3072]{0:T(1024)}, s32[3072]{0:T(1024)S(1)}, u32[]{:S(2)}) copy-start(s32[3072]{0:T(1024)S(1)} %fusion.82) | copy-start | bytes 36868
  38.2 13.9 copy-start.19
  184.4 5.6 copy-start.22
  184.4 35.5 %copy-start.28 = (f32[1024,2]{0,1:T(2,128)S(1)}, f32[1024,2]{0,1:T(2,128)}, u32[]{:S(2)}) copy-start(f32[1024,2]{0,1:T(2,128)} %param.21) | copy-start | bytes 24580
  184.4 76.0 %all-to-all-start.1 = ((bf16[4,4,192,1024]{3,2,1,0:T(8,128)(2,1)}), bf16[4,4,192,1024]{3,2,1,0:T(8,128)(2,1)}, u32[]{:S(2)}, u32[]{:S(2)}) async-start(bf16[4,4,192,1024]{3,2,1,0:T(8,128)(2,1)} %copy.91), calls=%async_computation.1 | async-start | bytes 12582912 | tf_op jit(solution)/shard_map/all_to_all | solution.py:89
  190.6 84.4 %copy-start.13 = (s32[2048]{0:T(1024)}, s32[2048]{0:T(1024)S(1)}, u32[]{:S(2)}) copy-start(s32[2048]{0:T(1024)S(1)} %eq.58) | copy-start | bytes 24580
  196.8 14.6 copy-start.15
  220.2 70.6 %copy-start.9 = (f32[1024,2]{1,0:T(8,128)}, f32[1024,2]{1,0:T(8,128)S(1)}, u32[]{:S(2)}) copy-start(f32[1024,2]{1,0:T(8,128)S(1)} %copy.85) | copy-start | bytes 24580
  220.2 54.7 %copy-start.23 = (pred[2048]{0:T(1024)(128)(4,1)}, pred[2048]{0:T(1024)(128)(4,1)S(1)}, u32[]{:S(2)}) copy-start(pred[2048]{0:T(1024)(128)(4,1)S(1)} %compare_and_fusion.3) | copy-start | bytes 6148
  220.2 54.7 %copy-start.17 = (s32[2048]{0:T(1024)}, s32[2048]{0:T(1024)S(1)}, u32[]{:S(2)}) copy-start(s32[2048]{0:T(1024)S(1)} %broadcast_clamp_fusion.1) | copy-start | bytes 24580
  329.4 79.0 %copy-start.5 = (bf16[1024,1024]{1,0:T(8,128)(2,1)S(1)}, bf16[1024,1024]{1,0:T(8,128)(2,1)}, u32[]{:S(2)}) copy-start(bf16[1024,1024]{1,0:T(8,128)(2,1)} %param.23) | copy-start | bytes 6291460
  329.4 75.7 %all-to-all-start.2 = ((bf16[4,4,192,1024]{3,2,1,0:T(8,128)(2,1)}), bf16[4,4,192,1024]{3,2,1,0:T(8,128)(2,1)}, u32[]{:S(2)}, u32[]{:S(2)}) async-start(bf16[4,4,192,1024]{3,2,1,0:T(8,128)(2,1)} %bitcast.162), calls=%async_computation.2 | async-start | bytes 12582912 | tf_op jit(solution)/shard_map/all_to_all | solution.py:86
  335.0 87.3 %copy-start.7 = (f32[1024,2]{1,0:T(8,128)}, f32[1024,2]{1,0:T(8,128)S(1)}, u32[]{:S(2)}) copy-start(f32[1024,2]{1,0:T(8,128)S(1)} %copy.92) | copy-start | bytes 24580
  405.2 23.9 %all-to-all-start.4 = ((f32[4,4,192]{2,1,0:T(4,128)}), f32[4,4,192]{2,1,0:T(4,128)S(1)}, u32[]{:S(2)}, u32[]{:S(2)}) async-start(f32[4,4,192]{2,1,0:T(4,128)} %reshape.205), calls=%async_computation.4 | async-start | bytes 32768 | tf_op jit(solution)/shard_map/all_to_all | solution.py:86
  429.1 75.6 %all-to-all-start.5 = ((bf16[4,4,192,1024]{3,2,1,0:T(8,128)(2,1)}), bf16[4,4,192,1024]{3,2,1,0:T(8,128)(2,1)}, u32[]{:S(2)}, u32[]{:S(2)}) async-start(bf16[4,4,192,1024]{3,2,1,0:T(8,128)(2,1)} %bitcast.161), calls=%async_computation.5 | async-start | bytes 12582912 | tf_op jit(solution)/shard_map/all_to_all | solution.py:86
  434.4 888.6 %reduce-scatter.15.cloned.1.call-start = ((), (), s32[]{:S(2)}) async-start(), calls=%async_computation.23 | async-start | bytes 37748736 | tf_op jit(solution)/shard_map/reduce_scatter | solution.py:98
  557.1 765.9 %reduce-scatter.13.cloned.1.call-start = ((), (), s32[]{:S(2)}) async-start(), calls=%async_computation.22 | async-start | bytes 37748736 | tf_op jit(solution)/shard_map/reduce_scatter | solution.py:98
  576.5 816.1 %reduce-scatter.17.cloned.1.call-start = ((), (), s32[]{:S(2)}) async-start(), calls=%async_computation.24 | async-start | bytes 37748736 | tf_op jit(solution)/shard_map/reduce_scatter | solution.py:98
  649.6 5.4 copy-start.27
  649.6 75.8 %all-to-all-start.3 = ((bf16[4,4,192,1024]{3,2,1,0:T(8,128)(2,1)}), bf16[4,4,192,1024]{3,2,1,0:T(8,128)(2,1)}, u32[]{:S(2)}, u32[]{:S(2)}) async-start(bf16[4,4,192,1024]{3,2,1,0:T(8,128)(2,1)} %copy.98), calls=%async_computation.3 | async-start | bytes 12582912 | tf_op jit(solution)/shard_map/all_to_all | solution.py:89
  725.4 28.7 %all-to-all-start.12 = ((f32[4,4,192]{2,1,0:T(4,128)}), f32[4,4,192]{2,1,0:T(4,128)S(1)}, u32[]{:S(2)}, u32[]{:S(2)}) async-start(f32[4,4,192]{2,1,0:T(4,128)} %copy.118), calls=%async_computation.18 | async-start | bytes 32768 | tf_op jit(solution)/shard_map/all_to_all | solution.py:89
  754.0 5.8 copy-start.10
  754.0 14.9 copy-start.14
  754.0 14.9 copy-start.16
  754.0 14.9 copy-start.1
  754.0 14.9 copy-start.12
  754.0 76.1 %all-to-all-start.6 = ((bf16[4,4,192,1024]{3,2,1,0:T(8,128)(2,1)}), bf16[4,4,192,1024]{3,2,1,0:T(8,128)(2,1)}, u32[]{:S(2)}, u32[]{:S(2)}) async-start(bf16[4,4,192,1024]{3,2,1,0:T(8,128)(2,1)} %copy.104), calls=%async_computation.6 | async-start | bytes 12582912 | tf_op jit(solution)/shard_map/all_to_all | solution.py:89
  830.1 78.1 %all-to-all-start.7 = ((f32[4,4,192]{2,1,0:T(4,128)}), f32[4,4,192]{2,1,0:T(4,128)S(1)}, u32[]{:S(2)}, u32[]{:S(2)}) async-start(f32[4,4,192]{2,1,0:T(4,128)} %reshape.209), calls=%async_computation.7 | async-start | bytes 32768 | tf_op jit(solution)/shard_map/all_to_all | solution.py:86
  883.8 13.9 copy-start.3
  883.8 13.9 copy-start.20
  883.8 13.9 copy-start.26
  985.2 25.2 %slice-start = ((s8[6291456]{0:T(1024)(128)(4,1)}), s8[2097152]{0:T(1024)(128)(4,1)S(1)}, s32[]{:S(2)}) async-start(s8[6291456]{0:T(1024)(128)(4,1)} %bitcast.166), calls=%async_computation.25 | async-start | bytes 4194304
  985.2 75.7 %all-to-all-start.8 = ((bf16[4,4,192,1024]{3,2,1,0:T(8,128)(2,1)}), bf16[4,4,192,1024]{3,2,1,0:T(8,128)(2,1)}, u32[]{:S(2)}, u32[]{:S(2)}) async-start(bf16[4,4,192,1024]{3,2,1,0:T(8,128)(2,1)} %bitcast.164), calls=%async_computation.8 | async-start | bytes 12582912 | tf_op jit(solution)/shard_map/all_to_all | solution.py:86
  990.6 681.3 %reduce-scatter.9.cloned.1.call-start = ((), (), s32[]{:S(2)}) async-start(), calls=%async_computation.20 | async-start | bytes 37748736 | tf_op jit(solution)/shard_map/reduce_scatter | solution.py:98
  990.6 19.8 slice-start.1
  1112.7 838.3 %reduce-scatter.7.cloned.1.call-start = ((), (), s32[]{:S(2)}) async-start(), calls=%async_computation.19 | async-start | bytes 37748736 | tf_op jit(solution)/shard_map/reduce_scatter | solution.py:98
  1132.2 1098.1 %reduce-scatter.11.cloned.1.call-start = ((), (), s32[]{:S(2)}) async-start(), calls=%async_computation.21 | async-start | bytes 37748736 | tf_op jit(solution)/shard_map/reduce_scatter | solution.py:98
  1152.5 46.9 %all-to-all-start.11 = ((f32[4,4,192]{2,1,0:T(4,128)}), f32[4,4,192]{2,1,0:T(4,128)S(1)}, u32[]{:S(2)}, u32[]{:S(2)}) async-start(f32[4,4,192]{2,1,0:T(4,128)} %copy.117), calls=%async_computation.17 | async-start | bytes 32768 | tf_op jit(solution)/shard_map/all_to_all | solution.py:89
  1199.4 5.6 copy-start.21
  1199.4 76.0 %all-to-all-start.10 = ((bf16[4,4,192,1024]{3,2,1,0:T(8,128)(2,1)}), bf16[4,4,192,1024]{3,2,1,0:T(8,128)(2,1)}, u32[]{:S(2)}, u32[]{:S(2)}) async-start(bf16[4,4,192,1024]{3,2,1,0:T(8,128)(2,1)} %copy.110), calls=%async_computation.10 | async-start | bytes 12582912 | tf_op jit(solution)/shard_map/all_to_all | solution.py:89
  1206.3 10.7 copy-start.8
  1217.0 12.1 copy-start.2
  1217.0 14.3 copy-start.18
  1229.0 14.0 copy-start.24
  1305.7 13.0 copy-start.4
  (2 other events, 8.1 us)
Sparse Core Ops, SparseCore 0:
  557.2 276.6 reduce-scatter.14
  836.8 276.4 reduce-scatter.12
  1116.1 276.4 reduce-scatter.16
  1395.3 276.4 reduce-scatter.8
  1674.6 276.4 reduce-scatter.6
  1953.8 276.4 reduce-scatter.10
where the time goes:
time: 2250 us; the launch traced here: 2240 us
  waiting for transfers between devices  1180 us (52%)
  matrix products  422 us (19%)
  local copies, waits for them, and re-layouts  298 us (13%)
  blocking collectives  152 us (7%)
  other arithmetic  121 us (5%)
  starting transfers between devices  51.8 us (2%)
    reduce_scatter x6, waiting for transfers between devices, layer_backward(): lax.psum_scatter(grad_part, 'dp', scatter_dimension=1, tiled=True)  907 us
    all_to_all x2, blocking collectives, exchange(): return lax.all_to_all(shaped, 'ep', 0, 0)  152 us
    all_to_all x6, waiting for transfers between devices, give_back(): returned = lax.all_to_all(expert_rows, 'ep', 0, 0)  143 us
    all_to_all x5, waiting for transfers between devices, exchange(): return lax.all_to_all(shaped, 'ep', 0, 0)  127 us
    gather x5, local copies, waits for them, and re-layouts, take_rows(): return jnp.take(values, row_tok, axis=0) * row_used[:, None]  73.2 us
    dot_general x2, matrix products, expert_backward(): jnp.einsum('secd,efd->escf', recv_dy, w_down, preferred_element_type=jnp....  65 us
    dot_general x2, matrix products, expert_forward(): jnp.einsum('escf,efd->secd', hidden, w_down, preferred_element_type=jnp.f...  55 us
  transfers between devices with their start and end apart: 17, of which 11 were waited for; matrix products, arithmetic and copies ran while one was open for 28% of the time, Pallas kernels for 0%

commit v1 on v0

v1 whole, which is shorter than its diff:
```python
import functools

import jax
import jax.numpy as jnp
from jax import lax
from jax.experimental import pallas as pl
from jax.experimental.pallas import tpu as pltpu
from jax.sharding import PartitionSpec as P

F32 = jnp.float32
BF16 = jnp.bfloat16
NN = (((1,), (0,)), ((), ()))
NT = (((1,), (1,)), ((), ()))
TN = (((0,), (0,)), ((), ()))
VMEM_LIMIT = 60 * 1024 * 1024


def mm(lhs, rhs, dims=NN):
    return lax.dot_general(lhs, rhs, dims, preferred_element_type=F32)


def params():
    return pltpu.CompilerParams(vmem_limit_bytes=VMEM_LIMIT, dimension_semantics=('arbitrary',))


def cost(flops, nbytes):
    return pl.CostEstimate(flops=int(flops), bytes_accessed=int(nbytes), transcendentals=0)


def plan_kernel(capacity, in_ref, row_ref, col_ref):
    n_tok = in_ref.shape[0]
    lane = lax.broadcasted_iota(jnp.int32, (n_tok, 128), 1)
    earlier = (lax.broadcasted_iota(jnp.int32, (n_tok, n_tok), 0)
               > lax.broadcasted_iota(jnp.int32, (n_tok, n_tok), 1))
    lower = jnp.where(earlier, 1.0, 0.0).astype(BF16)
    table = jnp.zeros((n_tok, 128), F32)
    for layer in range(2):
        ids = [in_ref[:, 2 * layer + j:2 * layer + j + 1] for j in range(2)]
        hot = [jnp.where(lane == i.astype(jnp.int32), 1.0, 0.0) for i in ids]
        count = mm(lower, (hot[0] + hot[1]).astype(BF16))
        for j in range(2):
            row = ids[j] * float(capacity) + jnp.sum(count * hot[j], axis=1, keepdims=True)
            table = jnp.where(lane == 2 * layer + j, row, table)
            table = jnp.where(lane == 4 + 2 * layer + j, in_ref[:, 4 + 2 * layer + j:5 + 2 * layer + j], table)
    col_ref[...] = table
    row_ref[...] = jnp.transpose(table)[:8]


def make_plan(packed, capacity):
    n_tok = packed.shape[0]
    return pl.pallas_call(
        functools.partial(plan_kernel, capacity),
        out_shape=(jax.ShapeDtypeStruct((8, n_tok), F32), jax.ShapeDtypeStruct((n_tok, 128), F32)),
        compiler_params=pltpu.CompilerParams(vmem_limit_bytes=VMEM_LIMIT),
        cost_estimate=cost(4 * n_tok * n_tok * 128, 1 << 20), name='plan')(packed)


def pick_kernel(layer, with_gate, base_ref, plan_ref, tok_ref, out_ref, *gate_out):
    n_exp, _, cap, dim = out_ref.shape
    n_rows, n_tok = n_exp * cap, tok_ref.shape[1]
    send_row = base_ref[0] + lax.broadcasted_iota(jnp.int32, (n_rows, n_tok), 0)
    hits = [plan_ref[0, 2 * layer + j:2 * layer + j + 1, :].astype(jnp.int32) == send_row for j in range(2)]
    select = jnp.where(hits[0] | hits[1], 1.0, 0.0).astype(BF16)
    out_ref[:, 0] = mm(select, tok_ref[0]).astype(BF16).reshape(n_exp, cap, dim)
    if with_gate:
        gates = [plan_ref[0, 4 + 2 * layer + j:5 + 2 * layer + j, :] for j in range(2)]
        picked = jnp.sum(jnp.where(hits[0], gates[0], 0.0) + jnp.where(hits[1], gates[1], 0.0), axis=1, keepdims=True)
        gate_out[0][:, 0] = jnp.broadcast_to(picked, (n_rows, 128)).reshape(n_exp, cap, 128)


def pick_rows(tokens, plans, place, layer, n_exp, cap, with_gate=False):
    n_src, n_tok, dim = tokens.shape
    out_shape = [jax.ShapeDtypeStruct((n_exp, n_src, cap, dim), BF16)]
    out_specs = [pl.BlockSpec((n_exp, 1, cap, dim), lambda s, _: (0, s, 0, 0))]
    if with_gate:
        out_shape.append(jax.ShapeDtypeStruct((n_exp, n_src, cap, 128), F32))
        out_specs.append(pl.BlockSpec((n_exp, 1, cap, 128), lambda s, _: (0, s, 0, 0)))
    picked = pl.pallas_call(
        functools.partial(pick_kernel, layer, with_gate),
        out_shape=out_shape,
        grid_spec=pltpu.PrefetchScalarGridSpec(
            num_scalar_prefetch=1, grid=(n_src,),
            in_specs=[pl.BlockSpec((1, 8, n_tok), lambda s, _: (s, 0, 0)),
                      pl.BlockSpec((1, n_tok, dim), lambda s, _: (s, 0, 0))],
            out_specs=out_specs),
        compiler_params=params(),
        cost_estimate=cost(2 * n_src * n_exp * cap * n_tok * dim, tokens.size * 4), name='pick')(place, plans, tokens)
    return picked if with_gate else picked[0]


def ffn_kernel(chunk, _, x_ref, w1_ref, w3_ref, w2_ref, out_ref, hid_ref):
    rows = x_ref.shape[1] * x_ref.shape[2]
    x = x_ref[0].reshape(rows, x_ref.shape[3])

    def step(c, carry):
        cols = pl.ds(pl.multiple_of(c * chunk, chunk), chunk)
        pre_one = mm(x, w1_ref[0, :, cols])
        pre_three = mm(x, w3_ref[0, :, cols])
        hid_ref[:, cols] = (pre_one * jax.nn.sigmoid(pre_one) * pre_three).astype(BF16)
        return carry

    lax.fori_loop(0, hid_ref.shape[1] // chunk, step, 0)
    out = mm(hid_ref[...], w2_ref[0])
    out_ref[:, 0] = out.astype(BF16).reshape(out_ref.shape[0], out_ref.shape[2], out_ref.shape[3])


def ffn(rows_x, place, w1, w3, w2, n_grp, pick_group):
    n_exp, _, cap, dim = rows_x.shape
    hid = w1.shape[2]
    group = (lambda e, p: (e, p[1], 0, 0)) if pick_group else (lambda e, p: (e, 0, 0, 0))
    whole = lambda e, p: (e, 0, 0)
    n_rows = n_exp * n_grp * cap
    return pl.pallas_call(
        functools.partial(ffn_kernel, 512),
        out_shape=jax.ShapeDtypeStruct((n_grp, n_exp, cap, dim), BF16),
        grid_spec=pltpu.PrefetchScalarGridSpec(
            num_scalar_prefetch=1, grid=(n_exp,),
            in_specs=[pl.BlockSpec((1, n_grp, cap, dim), group),
                      pl.BlockSpec((1, dim, hid), whole), pl.BlockSpec((1, dim, hid), whole),
                      pl.BlockSpec((1, hid, dim), whole)],
            out_specs=pl.BlockSpec((n_grp, 1, cap, dim), lambda e, p: (0, e, 0, 0)),
            scratch_shapes=[pltpu.VMEM((n_grp * cap, hid), BF16)]),
        compiler_params=params(),
        cost_estimate=cost(6 * n_rows * dim * hid, 6 * n_exp * dim * hid + 4 * n_rows * dim),
        name='ffn')(place, rows_x, w1, w3, w2)


def act_kernel(chunk, own, _, x_ref, dy_ref, gate_ref, w1_ref, w3_ref, w2_ref, da1_ref, da3_ref, h_ref, *own_refs):
    n_grp, cap, dim = x_ref.shape[1:]
    rows = n_grp * cap
    hid = w1_ref.shape[2]
    x = x_ref[0].reshape(rows, dim)
    dy = dy_ref[0].reshape(rows, dim)
    gate = gate_ref[0].reshape(rows, 128)[:, :1]

    def step(c, gate_grad):
        cols = pl.ds(pl.multiple_of(c * chunk, chunk), chunk)
        pre_one = mm(x, w1_ref[0, :, cols])
        pre_three = mm(x, w3_ref[0, :, cols])
        back = mm(dy, w2_ref[0, cols, :], NT)
        sig = jax.nn.sigmoid(pre_one)
        act = pre_one * sig
        hidden = (act * pre_three).astype(BF16)
        d_hidden = gate * back
        d_one = d_hidden * pre_three * sig * (1.0 + pre_one * (1.0 - sig))
        h_ref[0, :, :, cols] = hidden.reshape(n_grp, cap, chunk)
        da1_ref[0, :, :, cols] = d_one.astype(BF16).reshape(n_grp, cap, chunk)
        da3_ref[0, :, :, cols] = (d_hidden * act).astype(BF16).reshape(n_grp, cap, chunk)
        if own:
            gate_grad = gate_grad + jnp.sum(hidden.astype(F32) * back, axis=1, keepdims=True)
        return gate_grad

    gate_grad = lax.fori_loop(0, hid // chunk, step, jnp.zeros((rows, 1), F32))
    if own:
        du_ref, dgate_ref = own_refs
        dgate_ref[:, 0] = jnp.broadcast_to(gate_grad, (rows, 128)).reshape(n_grp, cap, 128)
        du = mm(da1_ref[0].reshape(rows, hid), w1_ref[0], NT) + mm(da3_ref[0].reshape(rows, hid), w3_ref[0], NT)
        du_ref[:, 0] = du.astype(BF16).reshape(n_grp, cap, dim)


def act(rows_x, rows_dy, gates, place, w1, w3, w2, n_grp, own):
    n_exp, _, cap, dim = rows_x.shape
    hid = w1.shape[2]
    group = (lambda e, p: (e, p[1], 0, 0)) if own else (lambda e, p: (e, 1 - p[1], 0, 0))
    whole = lambda e, p: (e, 0, 0)
    mine = lambda e, p: (e, 0, 0, 0)
    back = lambda e, p: (0, e, 0, 0)
    out_shape = [jax.ShapeDtypeStruct((n_exp, n_grp, cap, hid), BF16)] * 3
    out_specs = [pl.BlockSpec((1, n_grp, cap, hid), mine)] * 3
    if own:
        out_shape += [jax.ShapeDtypeStruct((n_grp, n_exp, cap, dim), BF16),
                      jax.ShapeDtypeStruct((n_grp, n_exp, cap, 128), F32)]
        out_specs += [pl.BlockSpec((n_grp, 1, cap, dim), back), pl.BlockSpec((n_grp, 1, cap, 128), back)]
    n_rows = n_exp * n_grp * cap
    return pl.pallas_call(
        functools.partial(act_kernel, 512, own),
        out_shape=out_shape,
        grid_spec=pltpu.PrefetchScalarGridSpec(
            num_scalar_prefetch=1, grid=(n_exp,),
            in_specs=[pl.BlockSpec((1, n_grp, cap, dim), group), pl.BlockSpec((1, n_grp, cap, dim), group),
                      pl.BlockSpec((1, n_grp, cap, 128), group),
                      pl.BlockSpec((1, dim, hid), whole), pl.BlockSpec((1, dim, hid), whole),
                      pl.BlockSpec((1, hid, dim), whole)],
            out_specs=out_specs),
        compiler_params=params(),
        cost_estimate=cost((10 if own else 6) * n_rows * dim * hid, 6 * n_exp * dim * hid + 8 * n_rows * hid),
        name='act_own' if own else 'act_other')(place, rows_x, rows_dy, gates, w1, w3, w2)


def dw_kernel(_, xs_ref, xo_ref, dys_ref, dyo_ref, gs_ref, go_ref, a1s_ref, a1o_ref, a3s_ref, a3o_ref, hs_ref, ho_ref,
              dw1_ref, dw3_ref, dw2_ref):
    def flat(ref):
        return ref[0].reshape(ref.shape[1] * ref.shape[2], ref.shape[3])

    xs, xo = flat(xs_ref), flat(xo_ref)
    dw1_ref[0] = mm(xs, flat(a1s_ref), TN) + mm(xo, flat(a1o_ref), TN)
    dw3_ref[0] = mm(xs, flat(a3s_ref), TN) + mm(xo, flat(a3o_ref), TN)
    gdy_s = (flat(gs_ref)[:, :1] * flat(dys_ref).astype(F32)).astype(BF16)
    gdy_o = (flat(go_ref)[:, :1] * flat(dyo_ref).astype(F32)).astype(BF16)
    dw2_ref[0] = mm(flat(hs_ref), gdy_s, TN) + mm(flat(ho_ref), gdy_o, TN)


def dweights(rows_x, rows_dy, gates, place, acts_own, acts_other, n_grp, n_dp):
    n_exp, _, cap, dim = rows_x.shape
    hid = acts_own[0].shape[3]
    dim_part, hid_part = dim // n_dp, hid // n_dp
    x_spec = [pl.BlockSpec((1, n_grp, cap, dim_part), lambda e, p: (e, p[1], 0, p[1])),
              pl.BlockSpec((1, n_grp, cap, dim_part), lambda e, p: (e, 1 - p[1], 0, p[1]))]
    both = lambda width: [pl.BlockSpec((1, n_grp, cap, width), lambda e, p: (e, p[1], 0, 0)),
                          pl.BlockSpec((1, n_grp, cap, width), lambda e, p: (e, 1 - p[1], 0, 0))]
    a_spec = pl.BlockSpec((1, n_grp, cap, hid), lambda e, p: (e, 0, 0, 0))
    h_spec = pl.BlockSpec((1, n_grp, cap, hid_part), lambda e, p: (e, 0, 0, p[1]))
    n_rows = n_exp * n_grp * cap
    up = jax.ShapeDtypeStruct((n_exp, dim_part, hid), F32)
    down = jax.ShapeDtypeStruct((n_exp, hid_part, dim), F32)
    whole = lambda e, p: (e, 0, 0)
    (a1s, a3s, hs), (a1o, a3o, ho) = acts_own, acts_other
    return pl.pallas_call(
        dw_kernel,
        out_shape=[up, up, down],
        grid_spec=pltpu.PrefetchScalarGridSpec(
            num_scalar_prefetch=1, grid=(n_exp,),
            in_specs=x_spec + both(dim) + both(128) + [a_spec] * 4 + [h_spec] * 2,
            out_specs=[pl.BlockSpec((1, dim_part, hid), whole)] * 2 + [pl.BlockSpec((1, hid_part, dim), whole)]),
        compiler_params=params(),
        cost_estimate=cost(6 * n_rows * dim * hid, 10 * n_rows * hid + 6 * n_exp * dim * hid),
        name='dweights')(place, rows_x, rows_x, rows_dy, rows_dy, gates, gates, a1s, a1o, a3s, a3o, hs, ho)


def hot_rows(plan_ref, col, n_rows):
    row = lax.broadcasted_iota(jnp.int32, (plan_ref.shape[0], n_rows), 1)
    return plan_ref[:, col:col + 1].astype(jnp.int32) == row


def mix_kernel(layer, x_ref, plan_ref, rows_ref, out_ref):
    total = None
    for j in range(2):
        hit = jnp.where(hot_rows(plan_ref, 2 * layer + j, rows_ref.shape[0]), 1.0, 0.0).astype(BF16)
        gate = plan_ref[:, 4 + 2 * layer + j:5 + 2 * layer + j]
        term = gate * mm(hit, rows_ref[...])
        total = term if total is None else total + term
    out_ref[...] = (x_ref[...].astype(F32) + total).astype(BF16)


def add_kernel(layer, dy_ref, plan_ref, rows_ref, dgate_ref, out_ref, gate_ref):
    n_rows = rows_ref.shape[0]
    hits = [hot_rows(plan_ref, 2 * layer + j, n_rows) for j in range(2)]
    hit = jnp.where(hits[0] | hits[1], 1.0, 0.0).astype(BF16)
    out_ref[...] = (dy_ref[...].astype(F32) + mm(hit, rows_ref[...])).astype(BF16)
    lane = lax.broadcasted_iota(jnp.int32, gate_ref.shape, 1)
    grads = [jnp.sum(jnp.where(h, dgate_ref[0:1, :], 0.0), axis=1, keepdims=True) for h in hits]
    gate_ref[...] = jnp.where(lane == 0, grads[0], jnp.where(lane == 1, grads[1], 0.0))


def combine(layer, x_in, plan_col, rows, dgate_rows=None):
    n_tok, dim = x_in.shape
    n_rows = rows.shape[0]
    tile = 256
    specs = [pl.BlockSpec((tile, dim), lambda t: (t, 0)), pl.BlockSpec((tile, 128), lambda t: (t, 0)),
             pl.BlockSpec((n_rows, dim), lambda t: (0, 0))]
    out = jax.ShapeDtypeStruct((n_tok, dim), BF16)
    est = cost(4 * n_tok * n_rows * dim, 2 * n_rows * dim)
    if dgate_rows is None:
        return pl.pallas_call(
            functools.partial(mix_kernel, layer), out_shape=out, grid=(n_tok // tile,),
            in_specs=specs, out_specs=specs[0], compiler_params=params(), cost_estimate=est,
            name='mix')(x_in, plan_col, rows)
    grad_x, dgate = pl.pallas_call(
        functools.partial(add_kernel, layer),
        out_shape=(out, jax.ShapeDtypeStruct((n_tok, 128), F32)), grid=(n_tok // tile,),
        in_specs=specs + [pl.BlockSpec((1, n_rows), lambda t: (0, 0))],
        out_specs=(specs[0], specs[1]), compiler_params=params(), cost_estimate=est,
        name='add_back')(x_in, plan_col, rows, dgate_rows)
    return grad_x, dgate[:, :2]


def solution(mesh):
    n_ep, n_dp = mesh.shape['ep'], mesh.shape['dp']
    tok_spec = P(('pod', 'dp', 'ep'), None)
    weight_spec = P('ep', None, None)
    grad_spec = P(('pod', 'ep'), 'dp', None)

    def local_step(x_start, route_a, route_b, gate_a, gate_b, grad_out, w1_a, w3_a, w2_a, w1_b, w3_b, w2_b):
        n_tok, dim = x_start.shape
        top_k = route_a.shape[1]
        n_local = w1_a.shape[0]
        n_experts = n_local * n_ep
        cap = 3 * n_tok * top_k // (2 * n_experts)
        ep_i, dp_i = lax.axis_index('ep'), lax.axis_index('dp')
        place = jnp.stack([ep_i * (n_local * cap), dp_i]).astype(jnp.int32)

        packed = jnp.concatenate([route_a.astype(F32), route_b.astype(F32), gate_a, gate_b], axis=1)
        plan_row, plan_col = make_plan(packed, cap)
        plans = lax.all_gather(plan_row, ('dp', 'ep'))
        plans_own = lax.dynamic_slice_in_dim(plans, dp_i * n_ep, n_ep, 0)

        def give_back(rows):
            returned = lax.all_to_all(rows, 'ep', 0, 0)
            return returned.reshape((n_experts * cap,) + rows.shape[3:])

        def experts_own(layer, rows_x, grads, weights):
            rows_dy, gates = pick_rows(grads, plans, place, layer, n_local, cap, with_gate=True)
            return rows_dy, gates, act(rows_x, rows_dy, gates, place, *weights, n_ep, True)

        def finish(layer, rows_x, grad_in, weights, rows_dy, gates, acts):
            da1, da3, h, du, dgate = acts
            other = act(rows_x, rows_dy, gates, place, *weights, n_ep, False)
            back = (give_back(du), give_back(dgate[..., 0]))
            dws = lambda acts_other: dweights(rows_x, rows_dy, gates, place, (da1, da3, h), acts_other, n_ep, n_dp)
            if layer == 0:
                (du_back, dgate_back), sums = hold((back, tuple(dws(other))))
            else:
                (du_back, dgate_back), other = hold((back, tuple(other)))
                sums = dws(other)
            grad_x, dgate_tok = combine(layer, grad_in, plan_col, du_back, dgate_back.reshape(1, -1))
            return grad_x, dgate_tok, sums

        hold = lax.optimization_barrier
        every = ('dp', 'ep')
        weights_a, weights_b = (w1_a, w3_a, w2_a), (w1_b, w3_b, w2_b)
        rows_a = pick_rows(lax.all_gather(x_start, 'ep'), plans_own, place, 0, n_local, cap)
        out_a = ffn(rows_a, place, *weights_a, n_ep, False)
        x_mid = combine(0, x_start, plan_col, give_back(out_a))
        x_kept, grad_kept, x_mid = hold((x_start, grad_out, x_mid))
        rows_b = pick_rows(lax.all_gather(x_mid, every), plans, place, 1, n_local, cap)
        out_b = ffn(rows_b, place, *weights_b, n_ep, True)
        grads_b, out_b = hold((lax.all_gather(grad_kept, every), out_b))
        own_b = experts_own(1, rows_b, grads_b, weights_b)
        grad_mid, dgate_b, dws_b = finish(1, rows_b, grad_kept, weights_b, *own_b)
        rows_a_again = pick_rows(lax.all_gather(x_kept, every), plans, place, 0, n_local, cap)
        grads_a, dws_b, out_b = hold((lax.all_gather(grad_mid, every), tuple(dws_b), out_b))
        rows_dy, gates, acts_a = experts_own(0, rows_a_again, grads_a, weights_a)
        acts_a, back_b = hold((tuple(acts_a), give_back(out_b)))
        grad_x, dgate_a, dws_a = finish(0, rows_a_again, grad_mid, weights_a, rows_dy, gates, acts_a)
        x_final = combine(1, x_mid, plan_col, back_b)
        (dw1_b, dw3_b, dw2_b), (dw1_a, dw3_a, dw2_a) = dws_b, dws_a
        return (x_final, grad_x, dw1_a, dw3_a, dw2_a, dw1_b, dw3_b, dw2_b, dgate_a, dgate_b)

    return jax.shard_map(local_step, mesh=mesh,
                         in_specs=(tok_spec,) * 6 + (weight_spec,) * 6,
                         out_specs=(tok_spec, tok_spec) + (grad_spec,) * 6 + (tok_spec, tok_spec),
                         check_vma=False)
```

time: 2250 us -> 911 us (0.40)
  waiting for transfers between devices: 1180 us -> 194 us
  Pallas kernels: 0 us -> 560 us
  matrix products: 422 us -> 0 us
  local copies, waits for them, and re-layouts: 298 us -> 10.3 us
  other arithmetic: 121 us -> 2.82 us
  blocking collectives: 152 us -> 99.1 us
  starting transfers between devices: 51.8 us -> 19.9 us
    reduce_scatter x6 -> x0, waiting for transfers between devices: 907 us -> none  [layer_backward(): lax.psum_scatter(grad_part, 'dp', scatter_dimension=1, tiled=True)]
    pallas_call x0 -> x18, Pallas kernels: none -> 560 us  [the longest x4 229 us: act(): pl.pallas_call(functools.partial(act_kernel, 512, own), out_shape=out_sha...]
    dot_general x20 -> x0, matrix products: 422 us -> none  [the longest x2 65 us: expert_backward(): jnp.einsum('secd,efd->escf', recv_dy, w_down, preferred_element_type=jnp....]
    all_to_all x11 -> x4, waiting for transfers between devices: 269 us -> 26.8 us  [give_back(): returned = lax.all_to_all(rows, 'ep', 0, 0)]
    all_gather x0 -> x5, waiting for transfers between devices: none -> 165 us  [the longest x1 82.9 us: local_step(): lax.all_gather(x_mid, every)]
    gather x11 -> x0, local copies, waits for them, and re-layouts: 155 us -> none  [the longest x5 73.2 us: take_rows(): return jnp.take(values, row_tok, axis=0) * row_used[:, None]]
    all_to_all x2, blocking collectives: 152 us -> 83.4 us  [give_back(): returned = lax.all_to_all(rows, 'ep', 0, 0)]
    convert_element_type x8 -> x0, local copies, waits for them, and re-layouts: 68.1 us -> none  [the longest x2 21.2 us: mix_back(): mixed_sum = jnp.sum(gate_vals[:, :, None] * pair_out, axis=1)]
  transfers between devices with their start and end apart: 17 -> 9, of which waited for: 11 -> 6; matrix products, arithmetic and copies ran while one was open for 28% -> 1% of each run, Pallas kernels for 0% -> 53%
where the time goes in v1:
time: 911 us; the launch traced here: 900 us
  Pallas kernels  560 us (61%)
  waiting for transfers between devices  194 us (21%)
  blocking collectives  99.1 us (11%)
  starting transfers between devices  19.9 us (2%)
  between operations  14.4 us (2%)
  local copies, waits for them, and re-layouts  10.3 us (1%)
    pallas_call x4, Pallas kernels, act(): pl.pallas_call(functools.partial(act_kernel, 512, own), out_shape=out_sha...  229 us
    pallas_call x5, Pallas kernels, pick_rows(): pl.pallas_call(functools.partial(pick_kernel, layer, with_gate), out_shap...  91.1 us
    pallas_call x2, Pallas kernels, dweights(): pl.pallas_call(dw_kernel, out_shape=[up, up, down], grid_spec=pltpu.Prefe...  85.6 us
    all_to_all x2, blocking collectives, give_back(): returned = lax.all_to_all(rows, 'ep', 0, 0)  83.4 us
    all_gather x1, waiting for transfers between devices, local_step(): lax.all_gather(x_mid, every)  82.9 us
    pallas_call x2, Pallas kernels, ffn(): pl.pallas_call(functools.partial(ffn_kernel, 512), out_shape=jax.ShapeDty...  77.6 us
    pallas_call x2, Pallas kernels, combine(): pl.pallas_call(functools.partial(mix_kernel, layer), out_shape=out, grid=...  36.2 us
    all_gather x1, waiting for transfers between devices, local_step(): lax.all_gather(x_start, 'ep')  33.5 us
  transfers between devices with their start and end apart: 9, of which 6 were waited for; matrix products, arithmetic and copies ran while one was open for 1% of the time, Pallas kernels for 53%

profile of v1, /device:TPU:0, one launch (start us, length us, event | category | flops | bytes accessed | tf_op | source)
XLA Modules:
  0.0 900.1 jit_solution(13737534765660981295)
XLA Ops:
  7.2 0.7 all-gather.12.cloned.1.call-update
  8.0 0.7 convert_element_type.7
  8.7 0.7 convert_element_type.6
  9.4 0.7 pad_maximum_fusion
  10.1 1.0 copy.34.in_ref
  11.1 8.0 plan.1
  19.1 15.7 %all-gather = f32[64,1024]{1,0:T(8,128)S(1)} all-gather(f32[8,1024]{1,0:T(8,128)} %get-tuple-element.69), channel_id=2, replica_groups=mesh['pod'=1,'dp'=2,'ep'=4] {'dp','ep'}, dimensions={0}, use_global_device_ids=true | all-gather | bytes 294912 | tf_op jit(solution)/shard_map/all_gather | solution.py:294
  34.8 0.7 pad_add_fusion.base_ref._
  35.5 0.7 constant_dynamic-slice_fusion.plan_ref
  36.1 33.5 %all-gather.12.cloned.1.call-done = bf16[4096,1024]{1,0:T(8,128)(2,1)} async-done(((bf16[1024,1024]{1,0:T(8,128)(2,1)}), bf16[4096,1024]{1,0:T(8,128)(2,1)}) %all-gather.12.cloned.1.call-update) | async-done | bytes 8388624 | tf_op jit(solution)/shard_map/all_gather | solution.py:321
  69.6 11.2 %pick.5.x_ref = bf16[4,4,192,1024]{3,2,1,0:T(8,128)(2,1)} custom-call(s32[2]{0:T(128)} %pad_add_fusion.base_ref._, f32[4,8,1024]{2,1,0:T(8,128)} %constant_dynamic-slice_fusion.plan_ref, bf16[4,1024,1024]{2,1,0:T(8,128)(2,1)} %bitcast.30), custom_call_target="tpu_custom_call" | custom-call | flops 6442450944 | bytes 16777216 | tf_op jit(solution)/shard_map/pick/pallas_call | solution.py:78
  80.8 38.8 %ffn.2 = bf16[4,4,192,1024]{3,2,1,0:T(8,128)(2,1)} custom-call(s32[2]{0:T(128)} %pad_add_fusion.base_ref._, bf16[4,4,192,1024]{3,2,1,0:T(8,128)(2,1)} %pick.5.x_ref, bf16[4,1024,1536]{2,1,0:T(8,128)(2,1)} %w1_ref.11, bf16[4,1024,1536]{2,1,0:T(8,128)(2,1)} %w3_ref.11, bf16[4,1536,1024]{2,1,0:T(8,128)(2,1)} %w2_ref.11), custom_call_target="tpu_custom_call" | custom-call | flops 28991029248 | bytes 50331648 | tf_op jit(solution)/shard_map/ffn/pallas_call | solution.py:113
  119.5 77.0 %all_to_all.30 = bf16[4,4,192,1024]{3,2,1,0:T(8,128)(2,1)} all-to-all(bf16[4,4,192,1024]{3,2,1,0:T(8,128)(2,1)} %ffn.2), channel_id=1, replica_groups=mesh['pod'=1,'dp'=2,'ep'=4] {'ep'}, dimensions={0} | all-to-all | bytes 12582912 | tf_op jit(solution)/shard_map/all_to_all | solution.py:298
  196.5 18.1 %mix.2.x_ref = bf16[1024,1024]{1,0:T(8,128)(2,1)} custom-call(bf16[1024,1024]{1,0:T(8,128)(2,1)} %x_ref.1, f32[1024,128]{1,0:T(8,128)} %get-tuple-element.68.plan_ref, bf16[3072,1024]{1,0:T(8,128)(2,1)} %bitcast.16), custom_call_target="tpu_custom_call" | custom-call | flops 12884901888 | bytes 6291456 | tf_op jit(solution)/shard_map/mix/pallas_call | solution.py:264
  214.7 0.4 all-gather.18.cloned.1.call-start
  215.1 0.3 all-gather.18.cloned.1.call-update
  215.5 0.5 all-gather.14.cloned.1.call-update
  216.0 82.9 %all-gather.16.cloned.1.call-done = bf16[8192,1024]{1,0:T(8,128)(2,1)} async-done(((bf16[1024,1024]{1,0:T(8,128)(2,1)}), bf16[8192,1024]{1,0:T(8,128)(2,1)}) %all-gather.16.cloned.1.call-update) | async-done | bytes 16777232 | tf_op jit(solution)/shard_map/all_gather | solution.py:325
  298.9 19.3 %pick.7.x_ref.xs_ref.xo_ref = bf16[4,8,192,1024]{3,2,1,0:T(8,128)(2,1)} custom-call(s32[2]{0:T(128)} %pad_add_fusion.base_ref._, f32[8,8,1024]{2,1,0:T(8,128)} %bitcast.18, bf16[8,1024,1024]{2,1,0:T(8,128)(2,1)} %bitcast.28), custom_call_target="tpu_custom_call" | custom-call | flops 12884901888 | bytes 33554432 | tf_op jit(solution)/shard_map/pick/pallas_call | solution.py:78
  318.1 38.8 %ffn.3 = bf16[4,4,192,1024]{3,2,1,0:T(8,128)(2,1)} custom-call(s32[2]{0:T(128)} %pad_add_fusion.base_ref._, bf16[4,8,192,1024]{3,2,1,0:T(8,128)(2,1)} %pick.7.x_ref.xs_ref.xo_ref, bf16[4,1024,1536]{2,1,0:T(8,128)(2,1)} %w1_ref.9, bf16[4,1024,1536]{2,1,0:T(8,128)(2,1)} %w3_ref.9, bf16[4,1536,1024]{2,1,0:T(8,128)(2,1)} %w2_ref.9), custom_call_target="tpu_custom_call" | custom-call | flops 28991029248 | bytes 50331648 | tf_op jit(solution)/shard_map/ffn/pallas_call | solution.py:113
  357.0 27.8 %all-gather.18.cloned.1.call-done = bf16[8192,1024]{1,0:T(8,128)(2,1)} async-done(((bf16[1024,1024]{1,0:T(8,128)(2,1)}), bf16[8192,1024]{1,0:T(8,128)(2,1)}) %all-gather.18.cloned.1.call-update) | async-done | bytes 16777232 | tf_op jit(solution)/shard_map/all_gather | solution.py:327
  384.8 20.7 %pick.8 = (bf16[4,8,192,1024]{3,2,1,0:T(8,128)(2,1)}, f32[4,8,192,128]{3,2,1,0:T(8,128)}) custom-call(s32[2]{0:T(128)} %pad_add_fusion.base_ref._, f32[8,8,1024]{2,1,0:T(8,128)} %bitcast.19, bf16[8,1024,1024]{2,1,0:T(8,128)(2,1)} %bitcast.29), custom_call_target="tpu_custom_call" | custom-call | flops 12884901888 | bytes 33554432 | tf_op jit(solution)/shard_map/pick/pallas_call | solution.py:78
  405.5 68.8 %act_own.2 = (bf16[4,4,192,1536]{3,2,1,0:T(8,128)(2,1)}, bf16[4,4,192,1536]{3,2,1,0:T(8,128)(2,1)}, bf16[4,4,192,1536]{3,2,1,0:T(8,128)(2,1)}, bf16[4,4,192,1024]{3,2,1,0:T(8,128)(2,1)}, f32[4,4,192,128]{3,2,1,0:T(8,128)}) custom-call(s32[2]{0:T(128)} %pad_add_fusion.base_ref._, bf16[4,8,192,1024]{3,2,1,0:T(8,128)(2,1)} %pick.7.x_ref.xs_ref.xo_ref, ...), custom_call_target="tpu_custom_call" | custom-call | flops 48318382080 | bytes 75497472 | tf_op jit(solution)/shard_map/act_own/pallas_call | solution.py:175
  474.2 2.0 slice_reduce_fusion.1
  476.2 6.4 all_to_all.31
  482.6 5.2 all-to-all-start.1
  487.9 0.0 all-gather.20.cloned.1.call-start
  487.9 45.7 %act_other.2 = (bf16[4,4,192,1536]{3,2,1,0:T(8,128)(2,1)}, bf16[4,4,192,1536]{3,2,1,0:T(8,128)(2,1)}, bf16[4,4,192,1536]{3,2,1,0:T(8,128)(2,1)}) custom-call(s32[2]{0:T(128)} %pad_add_fusion.base_ref._, bf16[4,8,192,1024]{3,2,1,0:T(8,128)(2,1)} %pick.7.x_ref.xs_ref.xo_ref, bf16[4,8,192,1024]{3,2,1,0:T(8,128)(2,1)} %get-tuple-element.74.dy_ref.dys_ref.dyo_ref, ...), custom_call_target="tpu_custom_call" | custom-call | flops 28991029248 | bytes 75497472 | tf_op jit(solution)/shard_map/act_other/pallas_call | solution.py:175
  533.6 0.7 reshape.46
  534.3 23.9 %all-to-all-done.1 = bf16[4,4,192,1024]{3,2,1,0:T(8,128)(2,1)} async-done(((bf16[4,4,192,1024]{3,2,1,0:T(8,128)(2,1)}), bf16[4,4,192,1024]{3,2,1,0:T(8,128)(2,1)}, u32[]{:S(2)}, u32[]{:S(2)}) %all-to-all-start.1) | async-done | bytes 6291488 | tf_op jit(solution)/shard_map/all_to_all | solution.py:298
  558.2 16.1 %add_back.2 = (bf16[1024,1024]{1,0:T(8,128)(2,1)}, f32[1024,128]{1,0:T(8,128)}) custom-call(bf16[1024,1024]{1,0:T(8,128)(2,1)} %dy_ref, f32[1024,128]{1,0:T(8,128)} %get-tuple-element.68.plan_ref, bf16[3072,1024]{1,0:T(8,128)(2,1)} %bitcast.8.rows_ref, f32[1,3072]{1,0:T(1,128)} %bitcast.25), custom_call_target="tpu_custom_call" | custom-call | flops 12884901888 | bytes 6291456 | tf_op jit(solution)/shard_map/add_back/pallas_call | solution.py:268
  574.3 19.3 %pick.6.x_ref.xs_ref.xo_ref = bf16[4,8,192,1024]{3,2,1,0:T(8,128)(2,1)} custom-call(s32[2]{0:T(128)} %pad_add_fusion.base_ref._, f32[8,8,1024]{2,1,0:T(8,128)} %bitcast.20, bf16[8,1024,1024]{2,1,0:T(8,128)(2,1)} %bitcast.26), custom_call_target="tpu_custom_call" | custom-call | flops 12884901888 | bytes 33554432 | tf_op jit(solution)/shard_map/pick/pallas_call | solution.py:78
  593.7 42.8 %dweights.2 = (f32[4,512,1536]{2,1,0:T(8,128)}, f32[4,512,1536]{2,1,0:T(8,128)}, f32[4,768,1024]{2,1,0:T(8,128)}) custom-call(s32[2]{0:T(128)} %pad_add_fusion.base_ref._, bf16[4,8,192,1024]{3,2,1,0:T(8,128)(2,1)} %pick.7.x_ref.xs_ref.xo_ref, bf16[4,8,192,1024]{3,2,1,0:T(8,128)(2,1)} %pick.7.x_ref.xs_ref.xo_ref, ...), custom_call_target="tpu_custom_call" | custom-call | flops 28991029248 | bytes 84934656 | tf_op jit(solution)/shard_map/dweights/pallas_call | solution.py:218
  636.4 21.3 %all-gather.20.cloned.1.call-done = bf16[8192,1024]{1,0:T(8,128)(2,1)} async-done(((bf16[1024,1024]{1,0:T(8,128)(2,1)}), bf16[8192,1024]{1,0:T(8,128)(2,1)}) %all-gather.20.cloned.1.call-update) | async-done | bytes 16777232 | tf_op jit(solution)/shard_map/all_gather | solution.py:331
  657.7 5.4 all-to-all-start.3
  663.2 20.7 %pick.9 = (bf16[4,8,192,1024]{3,2,1,0:T(8,128)(2,1)}, f32[4,8,192,128]{3,2,1,0:T(8,128)}) custom-call(s32[2]{0:T(128)} %pad_add_fusion.base_ref._, f32[8,8,1024]{2,1,0:T(8,128)} %bitcast.21, bf16[8,1024,1024]{2,1,0:T(8,128)(2,1)} %bitcast.27), custom_call_target="tpu_custom_call" | custom-call | flops 12884901888 | bytes 33554432 | tf_op jit(solution)/shard_map/pick/pallas_call | solution.py:78
  683.9 68.9 %act_own.3 = (bf16[4,4,192,1536]{3,2,1,0:T(8,128)(2,1)}, bf16[4,4,192,1536]{3,2,1,0:T(8,128)(2,1)}, bf16[4,4,192,1536]{3,2,1,0:T(8,128)(2,1)}, bf16[4,4,192,1024]{3,2,1,0:T(8,128)(2,1)}, f32[4,4,192,128]{3,2,1,0:T(8,128)}) custom-call(s32[2]{0:T(128)} %pad_add_fusion.base_ref._, bf16[4,8,192,1024]{3,2,1,0:T(8,128)(2,1)} %pick.6.x_ref.xs_ref.xo_ref, ...), custom_call_target="tpu_custom_call" | custom-call | flops 48318382080 | bytes 75497472 | tf_op jit(solution)/shard_map/act_own/pallas_call | solution.py:175
  752.7 2.6 slice_reduce_fusion
  755.4 3.3 all-to-all-start.5
  758.7 0.8 copy.36
  759.4 2.8 all-to-all-done.5
  762.3 5.5 all-to-all-start.4
  767.8 45.5 %act_other.3 = (bf16[4,4,192,1536]{3,2,1,0:T(8,128)(2,1)}, bf16[4,4,192,1536]{3,2,1,0:T(8,128)(2,1)}, bf16[4,4,192,1536]{3,2,1,0:T(8,128)(2,1)}) custom-call(s32[2]{0:T(128)} %pad_add_fusion.base_ref._, bf16[4,8,192,1024]{3,2,1,0:T(8,128)(2,1)} %pick.6.x_ref.xs_ref.xo_ref, bf16[4,8,192,1024]{3,2,1,0:T(8,128)(2,1)} %get-tuple-element.95.dy_ref.dys_ref.dyo_ref, ...), custom_call_target="tpu_custom_call" | custom-call | flops 28991029248 | bytes 75497472 | tf_op jit(solution)/shard_map/act_other/pallas_call | solution.py:175
  813.3 18.1 %mix.3 = bf16[1024,1024]{1,0:T(8,128)(2,1)} custom-call(bf16[1024,1024]{1,0:T(8,128)(2,1)} %mix.2.x_ref, f32[1024,128]{1,0:T(8,128)} %get-tuple-element.68.plan_ref, bf16[3072,1024]{1,0:T(8,128)(2,1)} %bitcast.11.rows_ref), custom_call_target="tpu_custom_call" | custom-call | flops 12884901888 | bytes 6291456 | tf_op jit(solution)/shard_map/mix/pallas_call | solution.py:264
  831.4 42.8 %dweights.3 = (f32[4,512,1536]{2,1,0:T(8,128)}, f32[4,512,1536]{2,1,0:T(8,128)}, f32[4,768,1024]{2,1,0:T(8,128)}) custom-call(s32[2]{0:T(128)} %pad_add_fusion.base_ref._, bf16[4,8,192,1024]{3,2,1,0:T(8,128)(2,1)} %pick.6.x_ref.xs_ref.xo_ref, bf16[4,8,192,1024]{3,2,1,0:T(8,128)(2,1)} %pick.6.x_ref.xs_ref.xo_ref, ...), custom_call_target="tpu_custom_call" | custom-call | flops 28991029248 | bytes 84934656 | tf_op jit(solution)/shard_map/dweights/pallas_call | solution.py:218
  874.2 0.7 reshape.50
  874.9 16.3 %add_back.3 = (bf16[1024,1024]{1,0:T(8,128)(2,1)}, f32[1024,128]{1,0:T(8,128)}) custom-call(bf16[1024,1024]{1,0:T(8,128)(2,1)} %get-tuple-element.83.dy_ref, f32[1024,128]{1,0:T(8,128)} %get-tuple-element.68.plan_ref, bf16[3072,1024]{1,0:T(8,128)(2,1)} %bitcast.12.rows_ref, f32[1,3072]{1,0:T(1,128)} %bitcast.24), custom_call_target="tpu_custom_call" | custom-call | flops 12884901888 | bytes 6291456 | tf_op jit(solution)/shard_map/add_back/pallas_call | solution.py:268
  891.2 1.8 copy.35
  (12 shorter events, 0.2 us)
Async XLA Ops:
  7.2 62.4 %all-gather.12.cloned.1.call-start = ((), (), s32[]{:S(2)}) async-start(), calls=%async_computation.6 | async-start | bytes 10485760 | tf_op jit(solution)/shard_map/all_gather | solution.py:321
  7.9 290.9 %all-gather.16.cloned.1.call-start = ((), (), s32[]{:S(2)}) async-start(), calls=%async_computation.8 | async-start | bytes 18874368 | tf_op jit(solution)/shard_map/all_gather | solution.py:325
  34.8 46.0 %copy-start = (f32[64,1024]{1,0:T(8,128)}, f32[64,1024]{1,0:T(8,128)S(1)}, u32[]{:S(2)}) copy-start(f32[64,1024]{1,0:T(8,128)S(1)} %all-gather) | copy-start | bytes 786436
  214.7 170.1 %all-gather.18.cloned.1.call-start = ((), (), s32[]{:S(2)}) async-start(), calls=%async_computation.9 | async-start | bytes 18874368 | tf_op jit(solution)/shard_map/all_gather | solution.py:327
  215.4 358.9 %all-gather.14.cloned.1.call-start = ((), (), s32[]{:S(2)}) async-start(), calls=%async_computation.7 | async-start | bytes 18874368 | tf_op jit(solution)/shard_map/all_gather | solution.py:330
  482.6 75.6 %all-to-all-start.1 = ((bf16[4,4,192,1024]{3,2,1,0:T(8,128)(2,1)}), bf16[4,4,192,1024]{3,2,1,0:T(8,128)(2,1)}, u32[]{:S(2)}, u32[]{:S(2)}) async-start(bf16[4,4,192,1024]{3,2,1,0:T(8,128)(2,1)} %get-tuple-element.76), calls=%async_computation.1 | async-start | bytes 12582912 | tf_op jit(solution)/shard_map/all_to_all | solution.py:298
  487.9 169.8 %all-gather.20.cloned.1.call-start = ((), (), s32[]{:S(2)}) async-start(), calls=%async_computation.10 | async-start | bytes 18874368 | tf_op jit(solution)/shard_map/all_gather | solution.py:331
  657.7 95.0 %all-to-all-start.3 = ((bf16[4,4,192,1024]{3,2,1,0:T(8,128)(2,1)}), bf16[4,4,192,1024]{3,2,1,0:T(8,128)(2,1)}, u32[]{:S(2)}, u32[]{:S(2)}) async-start(bf16[4,4,192,1024]{3,2,1,0:T(8,128)(2,1)} %ffn.3), calls=%async_computation.3 | async-start | bytes 12582912 | tf_op jit(solution)/shard_map/all_to_all | solution.py:298
  683.9 74.8 %copy-start.1 = (f32[1024,128]{1,0:T(8,128)S(1)}, f32[1024,128]{1,0:T(8,128)}, u32[]{:S(2)}) copy-start(f32[1024,128]{1,0:T(8,128)} %get-tuple-element.125) | copy-start | bytes 1572868
  755.4 6.9 all-to-all-start.5
  762.3 112.6 %all-to-all-start.4 = ((bf16[4,4,192,1024]{3,2,1,0:T(8,128)(2,1)}), bf16[4,4,192,1024]{3,2,1,0:T(8,128)(2,1)}, u32[]{:S(2)}, u32[]{:S(2)}) async-start(bf16[4,4,192,1024]{3,2,1,0:T(8,128)(2,1)} %get-tuple-element.104), calls=%async_computation.4 | async-start | bytes 12582912 | tf_op jit(solution)/shard_map/all_to_all | solution.py:298
Sparse Core Ops, SparseCore 0:
  9.5 60.0 all-gather.11
  214.8 84.0 all-gather.15
  300.7 84.0 all-gather.17
  386.5 84.0 all-gather.13
  574.4 83.2 all-gather.19

commit v2 on v0

v2 whole, which is shorter than its diff:
```python
import functools

import jax
import jax.numpy as jnp
from jax import lax
from jax.experimental import pallas as pl
from jax.experimental.pallas import tpu as pltpu
from jax.sharding import PartitionSpec as P


F32 = jnp.float32
BF16 = jnp.bfloat16
NN = (((1,), (0,)), ((), ()))
NT = (((1,), (1,)), ((), ()))
TN = (((0,), (0,)), ((), ()))
VMEM_LIMIT = 60 * 1024 * 1024


def mm(lhs, rhs, dims=NN):
    return lax.dot_general(lhs, rhs, dims, preferred_element_type=F32)


def params(n_axes=1):
    return pltpu.CompilerParams(vmem_limit_bytes=VMEM_LIMIT, dimension_semantics=('arbitrary',) * n_axes)


def cost(flops, nbytes):
    return pl.CostEstimate(flops=int(flops), bytes_accessed=int(nbytes), transcendentals=0)


def plan_kernel(capacity, in_ref, row_ref, col_ref):
    n_tok = in_ref.shape[0]
    lane = lax.broadcasted_iota(jnp.int32, (n_tok, 128), 1)
    earlier = (lax.broadcasted_iota(jnp.int32, (n_tok, n_tok), 0)
               > lax.broadcasted_iota(jnp.int32, (n_tok, n_tok), 1))
    lower = jnp.where(earlier, 1.0, 0.0).astype(BF16)
    table = jnp.zeros((n_tok, 128), F32)
    for layer in range(2):
        ids = [in_ref[:, 2 * layer + j:2 * layer + j + 1] for j in range(2)]
        hot = [jnp.where(lane == i.astype(jnp.int32), 1.0, 0.0) for i in ids]
        count = mm(lower, (hot[0] + hot[1]).astype(BF16))
        for j in range(2):
            row = ids[j] * float(capacity) + jnp.sum(count * hot[j], axis=1, keepdims=True)
            table = jnp.where(lane == 2 * layer + j, row, table)
            table = jnp.where(lane == 4 + 2 * layer + j, in_ref[:, 4 + 2 * layer + j:5 + 2 * layer + j], table)
    col_ref[...] = table
    row_ref[...] = jnp.transpose(table)[:8]


def make_plan(packed, capacity):
    n_tok = packed.shape[0]
    return pl.pallas_call(
        functools.partial(plan_kernel, capacity),
        out_shape=(jax.ShapeDtypeStruct((8, n_tok), F32), jax.ShapeDtypeStruct((n_tok, 128), F32)),
        compiler_params=pltpu.CompilerParams(vmem_limit_bytes=VMEM_LIMIT),
        cost_estimate=cost(4 * n_tok * n_tok * 128, 1 << 20), name='plan')(packed)


def pick_into(layer, base_ref, plan_ref, tokens, out_ref, gate_refs):
    n_exp, _, cap, dim = out_ref.shape
    n_rows, n_tok = n_exp * cap, tokens.shape[0]
    send_row = base_ref[0] + lax.broadcasted_iota(jnp.int32, (n_rows, n_tok), 0)
    hits = [plan_ref[0, 2 * layer + j:2 * layer + j + 1, :].astype(jnp.int32) == send_row for j in range(2)]
    select = jnp.where(hits[0] | hits[1], 1.0, 0.0).astype(BF16)
    out_ref[:, 0] = mm(select, tokens).astype(BF16).reshape(n_exp, cap, dim)
    for gate_ref in gate_refs:
        gates = [plan_ref[0, 4 + 2 * layer + j:5 + 2 * layer + j, :] for j in range(2)]
        picked = jnp.sum(jnp.where(hits[0], gates[0], 0.0) + jnp.where(hits[1], gates[1], 0.0), axis=1, keepdims=True)
        gate_ref[:, 0] = jnp.broadcast_to(picked, (n_rows, 128)).reshape(n_exp, cap, 128)


def pick_kernel(layer, base_ref, plan_ref, tok_ref, out_ref, *gate_refs):
    pick_into(layer, base_ref, plan_ref, tok_ref[0], out_ref, gate_refs)


def pick_parts_kernel(layer, n_src, base_ref, plan_ref, *refs):
    tabs, (held, sem) = refs[:n_src], refs[-2:]
    out_ref, gate_refs = refs[n_src], refs[n_src + 1:-2]
    src = pl.program_id(0)

    def load(i):
        return pltpu.make_async_copy(tabs[i], held.at[i % 2], sem.at[i % 2])

    for i in range(n_src):
        @pl.when(src == i)
        def _():
            if i == 0:
                load(0).start()
            if i + 1 < n_src:
                load(i + 1).start()
            load(i).wait()

    pick_into(layer, base_ref, plan_ref, held[src % 2], out_ref, gate_refs)


def pick_rows(tokens, plans, place, layer, n_exp, cap, with_gate=False):
    split = isinstance(tokens, tuple)
    n_src = len(tokens) if split else tokens.shape[0]
    source = 2 + (n_src if split else 0)
    n_tok, dim = tokens[0].shape
    out_shape = [jax.ShapeDtypeStruct((n_exp, n_src, cap, dim), BF16)]
    out_specs = [pl.BlockSpec((n_exp, 1, cap, dim), lambda s, _: (0, s, 0, 0))]
    if with_gate:
        out_shape.append(jax.ShapeDtypeStruct((n_exp, n_src, cap, 128), F32))
        out_specs.append(pl.BlockSpec((n_exp, 1, cap, 128), lambda s, _: (0, s, 0, 0)))
    if split:
        kernel = functools.partial(pick_parts_kernel, layer, n_src)
        tok_specs = [pl.BlockSpec(memory_space=pltpu.HBM)] * n_src
        scratch = [pltpu.VMEM((2, n_tok, dim), BF16), pltpu.SemaphoreType.DMA((2,))]
    else:
        kernel = functools.partial(pick_kernel, layer)
        tok_specs = [pl.BlockSpec((1, n_tok, dim), lambda s, _: (s, 0, 0))]
        scratch = []
        tokens = (tokens,)
    picked = pl.pallas_call(
        kernel, out_shape=out_shape,
        grid_spec=pltpu.PrefetchScalarGridSpec(
            num_scalar_prefetch=1, grid=(n_src,),
            in_specs=[pl.BlockSpec((1, 8, n_tok), lambda s, p: (p[source + s], 0, 0))] + tok_specs,
            out_specs=out_specs, scratch_shapes=scratch),
        compiler_params=params(),
        cost_estimate=cost(2 * n_src * n_exp * cap * n_tok * dim, n_src * n_tok * dim * 4),
        name='pick_other' if split else 'pick')(place, plans, *tokens)
    return picked if with_gate else picked[0]


def flat(ref):
    return ref[0].reshape(ref.shape[1] * ref.shape[2], ref.shape[3])


def ffn_kernel(n_chunk, x_ref, w1_ref, w3_ref, w2_ref, out_ref, hid_ref):
    c = pl.program_id(1)
    x = flat(x_ref)
    chunk = w1_ref.shape[2]
    pre_one = mm(x, w1_ref[0])
    pre_three = mm(x, w3_ref[0])
    hid_ref[:, pl.ds(pl.multiple_of(c * chunk, chunk), chunk)] = (
        pre_one * jax.nn.sigmoid(pre_one) * pre_three).astype(BF16)

    @pl.when(c == n_chunk - 1)
    def _():
        out = mm(hid_ref[...], w2_ref[0])
        out_ref[:, 0] = out.astype(BF16).reshape(out_ref.shape[0], out_ref.shape[2], out_ref.shape[3])


def ffn(rows_x, w1, w3, w2, first, n_exp, chunk=512):
    _, n_grp, cap, dim = rows_x.shape
    hid = w1.shape[2]
    n_rows = n_exp * n_grp * cap
    up = pl.BlockSpec((1, dim, chunk), lambda e, c: (e + first, 0, c))
    return pl.pallas_call(
        functools.partial(ffn_kernel, hid // chunk),
        out_shape=jax.ShapeDtypeStruct((n_grp, n_exp, cap, dim), BF16),
        grid=(n_exp, hid // chunk),
        in_specs=[pl.BlockSpec((1, n_grp, cap, dim), lambda e, c: (e + first, 0, 0, 0)), up, up,
                  pl.BlockSpec((1, hid, dim), lambda e, c: (e + first, 0, 0))],
        out_specs=pl.BlockSpec((n_grp, 1, cap, dim), lambda e, c: (0, e, 0, 0)),
        scratch_shapes=[pltpu.VMEM((n_grp * cap, hid), BF16)],
        compiler_params=params(2),
        cost_estimate=cost(6 * n_rows * dim * hid, 6 * n_exp * dim * hid + 4 * n_rows * dim),
        name='ffn')(rows_x, w1, w3, w2)


def act_kernel(n_chunk, own, n_kept, x_ref, dy_ref, gate_ref, w1_ref, w3_ref, w2_ref, *refs):
    da1_ref, da3_ref, h_ref, *own_refs = refs[n_kept:]
    n_grp, cap, dim = x_ref.shape[1:]
    rows = n_grp * cap
    chunk = w1_ref.shape[2]
    c = pl.program_id(1)
    x, dy = flat(x_ref), flat(dy_ref)
    pre_one = mm(x, w1_ref[0])
    pre_three = mm(x, w3_ref[0])
    back = mm(dy, w2_ref[0], NT)
    sig = jax.nn.sigmoid(pre_one)
    act_one = pre_one * sig
    hidden = (act_one * pre_three).astype(BF16)
    d_hidden = flat(gate_ref)[:, :1] * back
    d_one = (d_hidden * pre_three * sig * (1.0 + pre_one * (1.0 - sig))).astype(BF16)
    d_three = (d_hidden * act_one).astype(BF16)
    h_ref[0] = hidden.reshape(n_grp, cap, chunk)
    da1_ref[0] = d_one.reshape(n_grp, cap, chunk)
    da3_ref[0] = d_three.reshape(n_grp, cap, chunk)
    if own:
        du_ref, dgate_ref, total_ref = own_refs

        @pl.when(c == 0)
        def _():
            total_ref[...] = jnp.zeros_like(total_ref)
            dgate_ref[...] = jnp.zeros_like(dgate_ref)

        gate_grad = jnp.sum(hidden.astype(F32) * back, axis=1, keepdims=True)
        dgate_ref[:, 0] += jnp.broadcast_to(gate_grad, (rows, 128)).reshape(n_grp, cap, 128)
        total_ref[...] += mm(d_one, w1_ref[0], NT) + mm(d_three, w3_ref[0], NT)

        @pl.when(c == n_chunk - 1)
        def _():
            du_ref[:, 0] = total_ref[...].astype(BF16).reshape(n_grp, cap, dim)


def act(rows_x, rows_dy, gates, w1, w3, w2, first, n_exp, own, kept=(), chunk=512):
    n_all, n_grp, cap, dim = rows_x.shape
    hid = w1.shape[2]
    n_rows = n_exp * n_grp * cap
    rows = lambda e, c: (e + first, 0, 0, 0)
    back = lambda e, c: (0, e, 0, 0)
    up = pl.BlockSpec((1, dim, chunk), lambda e, c: (e + first, 0, c))
    out_shape = [jax.ShapeDtypeStruct((n_all, n_grp, cap, hid), BF16)] * 3
    out_specs = [pl.BlockSpec((1, n_grp, cap, chunk), lambda e, c: (e + first, 0, 0, c))] * 3
    scratch = []
    if own:
        out_shape += [jax.ShapeDtypeStruct((n_grp, n_exp, cap, dim), BF16),
                      jax.ShapeDtypeStruct((n_grp, n_exp, cap, 128), F32)]
        out_specs += [pl.BlockSpec((n_grp, 1, cap, dim), back), pl.BlockSpec((n_grp, 1, cap, 128), back)]
        scratch = [pltpu.VMEM((n_grp * cap, dim), F32)]
    return pl.pallas_call(
        functools.partial(act_kernel, hid // chunk, own, len(kept)),
        out_shape=out_shape, grid=(n_exp, hid // chunk),
        in_specs=[pl.BlockSpec((1, n_grp, cap, dim), rows), pl.BlockSpec((1, n_grp, cap, dim), rows),
                  pl.BlockSpec((1, n_grp, cap, 128), rows), up, up,
                  pl.BlockSpec((1, chunk, dim), lambda e, c: (e + first, c, 0))]
        + [pl.BlockSpec(memory_space=pltpu.HBM)] * len(kept),
        out_specs=out_specs, scratch_shapes=scratch, compiler_params=params(2),
        input_output_aliases={6 + i: i for i in range(len(kept))},
        cost_estimate=cost((10 if own else 6) * n_rows * dim * hid, 6 * n_exp * dim * hid + 8 * n_rows * hid),
        name='act_own' if own else 'act_other')(rows_x, rows_dy, gates, w1, w3, w2, *kept)


def dw_kernel(_, xs_ref, xo_ref, dys_ref, dyo_ref, gs_ref, go_ref, a1s_ref, a1o_ref, a3s_ref, a3o_ref, hs_ref, ho_ref,
              dw1_ref, dw3_ref, dw2_ref, gdy_s_ref, gdy_o_ref):
    @pl.when(pl.program_id(1) == 0)
    def _():
        gdy_s_ref[...] = (flat(gs_ref)[:, :1] * flat(dys_ref).astype(F32)).astype(BF16)
        gdy_o_ref[...] = (flat(go_ref)[:, :1] * flat(dyo_ref).astype(F32)).astype(BF16)

    xs, xo = flat(xs_ref), flat(xo_ref)
    dw1_ref[0] = mm(xs, flat(a1s_ref), TN) + mm(xo, flat(a1o_ref), TN)
    dw3_ref[0] = mm(xs, flat(a3s_ref), TN) + mm(xo, flat(a3o_ref), TN)
    dw2_ref[0] = mm(flat(hs_ref), gdy_s_ref[...], TN) + mm(flat(ho_ref), gdy_o_ref[...], TN)


def dweights(own, other, place, n_dp, n_chunk=3):
    (xs, dys, gs, a1s, a3s, hs), (xo, dyo, go, a1o, a3o, ho) = own, other
    n_exp, n_grp, cap, dim = xs.shape
    hid = a1s.shape[3]
    dim_part, hid_part = dim // n_dp, hid // n_dp
    up_c, down_c = hid // n_chunk, hid_part // n_chunk
    n_rows = n_exp * n_grp * cap
    x_spec = pl.BlockSpec((1, n_grp, cap, dim_part), lambda e, c, p: (e, 0, 0, p[1]))
    rows = lambda width: pl.BlockSpec((1, n_grp, cap, width), lambda e, c, p: (e, 0, 0, 0))
    a_spec = pl.BlockSpec((1, n_grp, cap, up_c), lambda e, c, p: (e, 0, 0, c))
    h_spec = pl.BlockSpec((1, n_grp, cap, down_c), lambda e, c, p: (e, 0, 0, n_chunk * p[1] + c))
    up = jax.ShapeDtypeStruct((n_exp, dim_part, hid), F32)
    down = jax.ShapeDtypeStruct((n_exp, hid_part, dim), F32)
    return pl.pallas_call(
        dw_kernel,
        out_shape=[up, up, down],
        grid_spec=pltpu.PrefetchScalarGridSpec(
            num_scalar_prefetch=1, grid=(n_exp, n_chunk),
            in_specs=[x_spec] * 2 + [rows(dim)] * 2 + [rows(128)] * 2 + [a_spec] * 4 + [h_spec] * 2,
            out_specs=[pl.BlockSpec((1, dim_part, up_c), lambda e, c, p: (e, 0, c))] * 2
            + [pl.BlockSpec((1, down_c, dim), lambda e, c, p: (e, c, 0))],
            scratch_shapes=[pltpu.VMEM((n_grp * cap, dim), BF16)] * 2),
        compiler_params=params(2),
        cost_estimate=cost(6 * n_rows * dim * hid, 10 * n_rows * hid + 6 * n_exp * dim * hid),
        name='dweights')(place, xs, xo, dys, dyo, gs, go, a1s, a1o, a3s, a3o, hs, ho)


def hits_of(plan_ref, layer, n_rows, n_ep, part, n_part):
    row = lax.broadcasted_iota(jnp.int32, (1, n_rows), 1)
    if n_part > 1:
        run = n_rows // n_ep
        owner = sum((row >= run * i).astype(jnp.int32) for i in range(1, n_ep))
        row = row + (owner * (n_part - 1) + part) * run
    return [plan_ref[:, 2 * layer + j:2 * layer + j + 1].astype(jnp.int32) == row for j in range(2)]


def one_hot(hit):
    return jnp.where(hit, 1.0, 0.0).astype(BF16)


def mix_kernel(layer, n_ep, part, n_part, base_ref, plan_ref, rows_ref, out_ref, partial_ref=None):
    hits = hits_of(plan_ref, layer, rows_ref.shape[0], n_ep, part, n_part)
    total = None
    for j in range(2):
        term = plan_ref[:, 4 + 2 * layer + j:5 + 2 * layer + j] * mm(one_hot(hits[j]), rows_ref[...])
        total = term if total is None else total + term
    finish(total, base_ref, out_ref, partial_ref)


def add_kernel(layer, n_ep, part, n_part, base_ref, plan_ref, rows_ref, out_ref, partial_ref=None):
    hits = hits_of(plan_ref, layer, rows_ref.shape[0], n_ep, part, n_part)
    finish(mm(one_hot(hits[0] | hits[1]), rows_ref[...]), base_ref, out_ref, partial_ref)


def finish(total, base_ref, out_ref, partial_ref):
    if partial_ref is not None:
        total = partial_ref[...] + total
    if base_ref is None:
        out_ref[...] = total
    else:
        out_ref[...] = (base_ref[...].astype(F32) + total).astype(BF16)


def combine(kernel, layer, x_in, plan_col, parts, n_ep, tile=256):
    n_tok, dim = x_in.shape
    wide = pl.BlockSpec((tile, dim), lambda t: (t, 0))
    partial = None
    for part, rows in enumerate(parts):
        n_rows = rows.shape[0]
        last = part == len(parts) - 1
        args = [plan_col, rows]
        specs = [pl.BlockSpec((tile, 128), lambda t: (t, 0)), pl.BlockSpec((n_rows, dim), lambda t: (0, 0))]
        if last:
            args, specs = [x_in] + args, [wide] + specs
        if partial is not None:
            args, specs = args + [partial], specs + [wide]

        def body(*refs, last=last, part=part, have=partial is not None):
            refs = list(refs)
            base = refs.pop(0) if last else None
            plan_ref, rows_ref = refs[0], refs[1]
            kernel(layer, n_ep, part, len(parts), base, plan_ref, rows_ref, refs[-1], refs[2] if have else None)

        partial = pl.pallas_call(
            body, out_shape=jax.ShapeDtypeStruct((n_tok, dim), BF16 if last else F32), grid=(n_tok // tile,),
            in_specs=specs, out_specs=wide, compiler_params=params(1),
            cost_estimate=cost((4 if kernel is mix_kernel else 2) * n_tok * n_rows * dim, 2 * n_rows * dim),
            name='mix' if kernel is mix_kernel else 'add_back')(*args)
    return partial


def gate_kernel(layer, plan_ref, dgate_ref, out_ref):
    lane = lax.broadcasted_iota(jnp.int32, out_ref.shape, 1)
    hits = hits_of(plan_ref, layer, dgate_ref.shape[1], 1, 0, 1)
    grads = [jnp.sum(jnp.where(h, dgate_ref[...], 0.0), axis=1, keepdims=True) for h in hits]
    out_ref[...] = jnp.where(lane == 0, grads[0], jnp.where(lane == 1, grads[1], 0.0))


def gate_back(layer, plan_col, dgate_rows, tile=256):
    n_tok = plan_col.shape[0]
    spec = pl.BlockSpec((tile, 128), lambda t: (t, 0))
    return pl.pallas_call(
        functools.partial(gate_kernel, layer), out_shape=jax.ShapeDtypeStruct((n_tok, 128), F32),
        grid=(n_tok // tile,), in_specs=[spec, pl.BlockSpec(dgate_rows.shape, lambda t: (0, 0))],
        out_specs=spec, compiler_params=params(1), cost_estimate=cost(5e9, 1 << 20),
        name='gate_back')(plan_col, dgate_rows)[:, :2]


def solution(mesh):
    n_ep, n_dp = mesh.shape['ep'], mesh.shape['dp']
    tok_spec = P(('pod', 'dp', 'ep'), None)
    weight_spec = P('ep', None, None)
    grad_spec = P(('pod', 'ep'), 'dp', None)
    hold = lax.optimization_barrier
    swap_dp = [(0, 1), (1, 0)]
    swap_core = [(i, i ^ 1) for i in range(n_ep)]

    def local_step(x_start, route_a, route_b, gate_a, gate_b, grad_out, w1_a, w3_a, w2_a, w1_b, w3_b, w2_b):
        n_tok, _ = x_start.shape
        top_k = route_a.shape[1]
        n_local = w1_a.shape[0]
        n_experts = n_local * n_ep
        cap = 3 * n_tok * top_k // (2 * n_experts)
        half = n_local // 2
        ep_i, dp_i = lax.axis_index('ep'), lax.axis_index('dp')
        own_src = [dp_i * n_ep + i for i in range(n_ep)]
        far_src = [(1 - dp_i) * n_ep + jnp.bitwise_xor(ep_i, i) for i in (0, 2, 1, 3)]
        place = jnp.stack([ep_i * (n_local * cap), dp_i] + own_src + far_src).astype(jnp.int32)
        across = jnp.bitwise_xor(ep_i, 2)

        packed = jnp.concatenate([route_a.astype(F32), route_b.astype(F32), gate_a, gate_b], axis=1)
        plan_row, plan_col = make_plan(packed, cap)
        plans = lax.all_gather(plan_row, ('dp', 'ep'))

        def give_back(rows):
            returned = lax.all_to_all(rows, 'ep', 0, 0)
            return returned.reshape((-1,) + rows.shape[3:])

        def near(tokens):
            return lax.all_gather(tokens, 'ep')

        def cross(tokens, gathered):
            next_chip = lax.dynamic_index_in_dim(gathered, across, 0, False)
            return [lax.ppermute(t, 'dp', swap_dp) for t in (tokens, next_chip)]

        def far(crossed, after):
            crossed, _ = hold((tuple(crossed), after))
            return crossed + tuple(lax.ppermute(t, 'ep', swap_core) for t in crossed)

        def pick(tokens, layer, with_gate=False):
            return pick_rows(tokens, plans, place, layer, n_local, cap, with_gate)

        weights_a, weights_b = (w1_a, w3_a, w2_a), (w1_b, w3_b, w2_b)

        rows_a = pick(near(x_start), 0)
        out_a = [ffn(rows_a, *weights_a, i * half, half) for i in range(2)]
        back_a, out_a[1] = hold((give_back(out_a[0]), out_a[1]))
        x_mid = combine(mix_kernel, 0, x_start, plan_col, [back_a, give_back(out_a[1])], n_ep)

        x_kept, grad_kept, x_mid = hold((x_start, grad_out, x_mid))
        near_x = near(x_mid)
        far_x = cross(x_mid, near_x)
        rows_b = pick(near_x, 1)
        out_b = ffn(rows_b, *weights_b, 0, n_local)

        near_dy, out_b = hold((near(grad_kept), out_b))
        far_dy = cross(grad_kept, near_dy)
        dy_b, gates_b = pick(near_dy, 1, True)
        own_b = [act(rows_b, dy_b, gates_b, *weights_b, 0, half, True)]
        own_b.append(act(rows_b, dy_b, gates_b, *weights_b, half, n_local - half, True,
                           tuple(own_b[0][:3])))
        back_du, own_b[1] = hold((give_back(own_b[0][3]), tuple(own_b[1])))
        du_b = [back_du, give_back(own_b[1][3])]
        dgate_b = give_back(jnp.concatenate([o[4][..., 0] for o in own_b], axis=1))
        near_a = near(x_kept)
        far_a = cross(x_kept, near_a)
        rows_a2 = pick(near_a, 0)
        rows_b_far = pick(far(far_x, own_b[0][0]), 1)
        dy_b_far, gates_b_far = pick(far(far_dy, own_b[1][0]), 1, True)
        du_b[1], dgate_b, rows_a2, rows_b_far, dy_b_far = hold((du_b[1], dgate_b, rows_a2, rows_b_far, dy_b_far))
        grad_mid = combine(add_kernel, 1, grad_kept, plan_col, du_b, n_ep)
        dgate_b = gate_back(1, plan_col, dgate_b.reshape(1, -1))

        near_dx = near(grad_mid)
        other_b = act(rows_b_far, dy_b_far, gates_b_far, *weights_b, 0, n_local, False)
        near_dx, other_b, out_b = hold((near_dx, tuple(other_b), out_b))
        far_dx = cross(grad_mid, near_dx)
        dy_a, gates_a = pick(near_dx, 0, True)
        own_a = act(rows_a2, dy_a, gates_a, *weights_a, 0, n_local, True)
        back_b = give_back(out_b)
        own_a, back_b, other_b = hold((tuple(own_a), back_b, other_b))
        du_a = give_back(own_a[3])
        dgate_a = give_back(own_a[4][..., 0])
        x_final = combine(mix_kernel, 1, x_mid, plan_col, [back_b], n_ep)
        dws_b = dweights((rows_b, dy_b, gates_b) + tuple(own_b[1][:3]), (rows_b_far, dy_b_far, gates_b_far) + tuple(other_b),
                         place, n_dp)
        rows_a_far = pick(far(far_a, own_a[0]), 0)
        dy_a_far, gates_a_far = pick(far(far_dx, own_a[0]), 0, True)
        other_a = act(rows_a_far, dy_a_far, gates_a_far, *weights_a, 0, n_local, False)
        dws_a = dweights((rows_a2, dy_a, gates_a) + tuple(own_a[:3]), (rows_a_far, dy_a_far, gates_a_far) + tuple(other_a),
                         place, n_dp)
        du_a, dws_a, dws_b, x_final = hold((du_a, tuple(dws_a), tuple(dws_b), x_final))
        grad_x = combine(add_kernel, 0, grad_mid, plan_col, [du_a], n_ep)
        dgate_a = gate_back(0, plan_col, dgate_a.reshape(1, -1))
        return (x_final, grad_x) + tuple(dws_a) + tuple(dws_b) + (dgate_a, dgate_b)

    return jax.shard_map(local_step, mesh=mesh,
                         in_specs=(tok_spec,) * 6 + (weight_spec,) * 6,
                         out_specs=(tok_spec, tok_spec) + (grad_spec,) * 6 + (tok_spec, tok_spec),
                         check_vma=False)
```

time: 2250 us -> 895 us (0.40)
  waiting for transfers between devices: 1180 us -> 171 us
  Pallas kernels: 0 us -> 594 us
  matrix products: 422 us -> 0 us
  local copies, waits for them, and re-layouts: 298 us -> 26.4 us
  blocking collectives: 152 us -> 23.5 us
  other arithmetic: 121 us -> 2.15 us
    reduce_scatter x6 -> x0, waiting for transfers between devices: 907 us -> none  [layer_backward(): lax.psum_scatter(grad_part, 'dp', scatter_dimension=1, tiled=True)]
    pallas_call x0 -> x28, Pallas kernels: none -> 594 us  [the longest x5 225 us: act(): pl.pallas_call(functools.partial(act_kernel, hid // chunk, own, len(kept)...]
    dot_general x20 -> x0, matrix products: 422 us -> none  [the longest x2 65 us: expert_backward(): jnp.einsum('secd,efd->escf', recv_dy, w_down, preferred_element_type=jnp....]
    all_to_all x11 -> x7, waiting for transfers between devices: 269 us -> 32.9 us  [give_back(): returned = lax.all_to_all(rows, 'ep', 0, 0)]
    gather x11 -> x0, local copies, waits for them, and re-layouts: 155 us -> none  [the longest x5 73.2 us: take_rows(): return jnp.take(values, row_tok, axis=0) * row_used[:, None]]
    all_to_all x2 -> x1, blocking collectives: 152 us -> 6.65 us  [give_back(): returned = lax.all_to_all(rows, 'ep', 0, 0)]
    all_gather x0 -> x5, waiting for transfers between devices: none -> 88.5 us  [near(): return lax.all_gather(tokens, 'ep')]
    convert_element_type x8 -> x0, local copies, waits for them, and re-layouts: 68.1 us -> none  [the longest x2 21.2 us: mix_back(): mixed_sum = jnp.sum(gate_vals[:, :, None] * pair_out, axis=1)]
  transfers between devices with their start and end apart: 17 -> 28, of which waited for: 11 -> 7; matrix products, arithmetic and copies ran while one was open for 28% -> 3% of each run, Pallas kernels for 0% -> 60%
where the time goes in v2:
time: 895 us; the launch traced here: 884 us
  Pallas kernels  594 us (66%)
  waiting for transfers between devices  171 us (19%)
  starting transfers between devices  52.4 us (6%)
  local copies, waits for them, and re-layouts  26.4 us (3%)
  blocking collectives  23.5 us (3%)
  between operations  14.3 us (2%)
    pallas_call x5, Pallas kernels, act(): pl.pallas_call(functools.partial(act_kernel, hid // chunk, own, len(kept)...  225 us
    pallas_call x9, Pallas kernels, pick_rows(): pl.pallas_call(kernel, out_shape=out_shape, grid_spec=pltpu.PrefetchScala...  108 us
    pallas_call x2, Pallas kernels, dweights(): pl.pallas_call(dw_kernel, out_shape=[up, up, down], grid_spec=pltpu.Prefe...  95.8 us
    all_gather x5, waiting for transfers between devices, near(): return lax.all_gather(tokens, 'ep')  88.5 us
    pallas_call x3, Pallas kernels, ffn(): pl.pallas_call(functools.partial(ffn_kernel, hid // chunk), out_shape=jax...  78.7 us
    pallas_call x6, Pallas kernels, combine(): pl.pallas_call(body, out_shape=jax.ShapeDtypeStruct((n_tok, dim), BF16 if...  66.4 us
    ppermute x8, waiting for transfers between devices, cross(): return [lax.ppermute(t, 'dp', swap_dp) for t in (tokens, next_chip)]  47.7 us
    all_to_all x7, waiting for transfers between devices, give_back(): returned = lax.all_to_all(rows, 'ep', 0, 0)  32.9 us
  transfers between devices with their start and end apart: 28, of which 7 were waited for; matrix products, arithmetic and copies ran while one was open for 3% of the time, Pallas kernels for 60%

profile of v2, /device:TPU:0, one launch (start us, length us, event | category | flops | bytes accessed | tf_op | source)
XLA Modules:
  0.0 884.1 jit_solution(13983557005344907022)
XLA Ops:
  11.7 8.0 plan.1
  19.7 16.8 %all-gather = f32[64,1024]{1,0:T(8,128)} all-gather(f32[8,1024]{1,0:T(8,128)} %get-tuple-element.95), channel_id=2, replica_groups=mesh['pod'=1,'dp'=2,'ep'=4] {'dp','ep'}, dimensions={0}, use_global_device_ids=true | all-gather | bytes 294912 | tf_op jit(solution)/shard_map/all_gather | solution.py:373
  36.5 32.9 %all-gather.12.cloned.1.call-done = bf16[4096,1024]{1,0:T(8,128)(2,1)} async-done(((bf16[1024,1024]{1,0:T(8,128)(2,1)}), bf16[4096,1024]{1,0:T(8,128)(2,1)}) %all-gather.12.cloned.1.call-update) | async-done | bytes 8388624 | tf_op jit(solution)/shard_map/all_gather | solution.py:380
  69.4 11.2 %pick.5.x_ref = bf16[4,4,192,1024]{3,2,1,0:T(8,128)(2,1)} custom-call(s32[10]{0:T(128)} %stack.43.base_ref._, f32[8,8,1024]{2,1,0:T(8,128)} %bitcast.45, bf16[4,1024,1024]{2,1,0:T(8,128)(2,1)} %bitcast.55), custom_call_target="tpu_custom_call" | custom-call | flops 6442450944 | bytes 16777216 | tf_op jit(solution)/shard_map/pick/pallas_call | solution.py:115
  80.5 20.6 %ffn.3 = bf16[4,2,192,1024]{3,2,1,0:T(8,128)(2,1)} custom-call(bf16[4,4,192,1024]{3,2,1,0:T(8,128)(2,1)} %pick.5.x_ref, bf16[4,1024,1536]{2,1,0:T(8,128)(2,1)} %w1_ref.15, bf16[4,1024,1536]{2,1,0:T(8,128)(2,1)} %w3_ref.15, bf16[4,1536,1024]{2,1,0:T(8,128)(2,1)} %w2_ref.15), custom_call_target="tpu_custom_call" | custom-call | flops 14495514624 | bytes 25165824 | tf_op jit(solution)/shard_map/ffn/pallas_call | solution.py:151
  101.2 3.7 all-to-all-start
  104.9 20.7 %ffn.4 = bf16[4,2,192,1024]{3,2,1,0:T(8,128)(2,1)} custom-call(bf16[4,4,192,1024]{3,2,1,0:T(8,128)(2,1)} %pick.5.x_ref, bf16[4,1024,1536]{2,1,0:T(8,128)(2,1)} %w1_ref.15, bf16[4,1024,1536]{2,1,0:T(8,128)(2,1)} %w3_ref.15, bf16[4,1536,1024]{2,1,0:T(8,128)(2,1)} %w2_ref.15), custom_call_target="tpu_custom_call" | custom-call | flops 14495514624 | bytes 25165824 | tf_op jit(solution)/shard_map/ffn/pallas_call | solution.py:151
  125.5 16.2 %all-to-all-done = bf16[4,2,192,1024]{3,2,1,0:T(8,128)(2,1)S(1)} async-done(((bf16[4,2,192,1024]{3,2,1,0:T(8,128)(2,1)}), bf16[4,2,192,1024]{3,2,1,0:T(8,128)(2,1)S(1)}, u32[]{:S(2)}, u32[]{:S(2)}) %all-to-all-start) | async-done | bytes 3145760 | tf_op jit(solution)/shard_map/all_to_all | solution.py:376
  141.7 4.7 all-to-all-start.1
  146.4 9.9 %all-gather.14.cloned.1.call-start = ((), (), s32[]{:S(2)}) async-start(), calls=%async_computation.9 | async-start | bytes 10485760 | tf_op jit(solution)/shard_map/all_gather | solution.py:380
  156.3 10.4 %mix.3.refs_3_ = f32[1024,1024]{1,0:T(8,128)} custom-call(f32[1024,128]{1,0:T(8,128)} %get-tuple-element.96.refs_0_.refs_1_.plan_ref, bf16[1536,1024]{1,0:T(8,128)(2,1)} %bitcast.34), custom_call_target="tpu_custom_call" | custom-call | flops 6442450944 | bytes 3145728 | tf_op jit(solution)/shard_map/mix/pallas_call | solution.py:324
  166.7 16.7 %all-to-all-done.1 = bf16[4,2,192,1024]{3,2,1,0:T(8,128)(2,1)} async-done(((bf16[4,2,192,1024]{3,2,1,0:T(8,128)(2,1)}), bf16[4,2,192,1024]{3,2,1,0:T(8,128)(2,1)}, u32[]{:S(2)}, u32[]{:S(2)}) %all-to-all-start.1) | async-done | bytes 3145760 | tf_op jit(solution)/shard_map/all_to_all | solution.py:376
  183.4 11.1 %mix.4.refs_0_ = bf16[1024,1024]{1,0:T(8,128)(2,1)} custom-call(bf16[1024,1024]{1,0:T(8,128)(2,1)} %refs_0_.1, f32[1024,128]{1,0:T(8,128)} %get-tuple-element.96.refs_0_.refs_1_.plan_ref, bf16[1536,1024]{1,0:T(8,128)(2,1)} %bitcast.13.refs_2_, f32[1024,1024]{1,0:T(8,128)} %mix.3.refs_3_), custom_call_target="tpu_custom_call" | custom-call | flops 6442450944 | bytes 3145728 | tf_op jit(solution)/shard_map/mix/pallas_call | solution.py:324
  197.8 52.2 %all-gather.14.cloned.1.call-done = bf16[4096,1024]{1,0:T(8,128)(2,1)} async-done(((bf16[1024,1024]{1,0:T(8,128)(2,1)}), bf16[4096,1024]{1,0:T(8,128)(2,1)}) %all-gather.14.cloned.1.call-update) | async-done | bytes 8388624 | tf_op jit(solution)/shard_map/all_gather | solution.py:380
  250.1 3.1 dynamic-slice_bitcast_fusion.3
  254.6 11.7 %pick.6.x_ref.xs_ref = bf16[4,4,192,1024]{3,2,1,0:T(8,128)(2,1)} custom-call(s32[10]{0:T(128)} %stack.43.base_ref._, f32[8,8,1024]{2,1,0:T(8,128)} %bitcast.46, bf16[4,1024,1024]{2,1,0:T(8,128)(2,1)} %bitcast.40), custom_call_target="tpu_custom_call" | custom-call | flops 6442450944 | bytes 16777216 | tf_op jit(solution)/shard_map/pick/pallas_call | solution.py:115
  266.4 37.5 %ffn.5 = bf16[4,4,192,1024]{3,2,1,0:T(8,128)(2,1)} custom-call(bf16[4,4,192,1024]{3,2,1,0:T(8,128)(2,1)} %pick.6.x_ref.xs_ref, bf16[4,1024,1536]{2,1,0:T(8,128)(2,1)} %w1_ref.13, bf16[4,1024,1536]{2,1,0:T(8,128)(2,1)} %w3_ref.13, bf16[4,1536,1024]{2,1,0:T(8,128)(2,1)} %w2_ref.13), custom_call_target="tpu_custom_call" | custom-call | flops 28991029248 | bytes 50331648 | tf_op jit(solution)/shard_map/ffn/pallas_call | solution.py:151
  303.8 3.3 all-gather.16.cloned.1.call-done
  307.1 12.3 %pick.7 = (bf16[4,4,192,1024]{3,2,1,0:T(8,128)(2,1)}, f32[4,4,192,128]{3,2,1,0:T(8,128)}) custom-call(s32[10]{0:T(128)} %stack.43.base_ref._, f32[8,8,1024]{2,1,0:T(8,128)} %bitcast.47, bf16[4,1024,1024]{2,1,0:T(8,128)(2,1)} %bitcast.37), custom_call_target="tpu_custom_call" | custom-call | flops 6442450944 | bytes 16777216 | tf_op jit(solution)/shard_map/pick/pallas_call | solution.py:115
  319.4 35.9 %act_own.3 = (bf16[4,4,192,1536]{3,2,1,0:T(8,128)(2,1)}, bf16[4,4,192,1536]{3,2,1,0:T(8,128)(2,1)}, bf16[4,4,192,1536]{3,2,1,0:T(8,128)(2,1)}, bf16[4,2,192,1024]{3,2,1,0:T(8,128)(2,1)}, f32[4,2,192,128]{3,2,1,0:T(8,128)}) custom-call(bf16[4,4,192,1024]{3,2,1,0:T(8,128)(2,1)} %pick.6.x_ref.xs_ref, ...), custom_call_target="tpu_custom_call" | custom-call | flops 24159191040 | bytes 37748736 | tf_op jit(solution)/shard_map/act_own/pallas_call | solution.py:215
  355.3 5.1 all-to-all-start.2
  360.4 3.1 dynamic-slice_bitcast_fusion.2
  365.5 35.9 %act_own.4 = (bf16[4,4,192,1536]{3,2,1,0:T(8,128)(2,1)}, bf16[4,4,192,1536]{3,2,1,0:T(8,128)(2,1)}, bf16[4,4,192,1536]{3,2,1,0:T(8,128)(2,1)}, bf16[4,2,192,1024]{3,2,1,0:T(8,128)(2,1)}, f32[4,2,192,128]{3,2,1,0:T(8,128)}) custom-call(bf16[4,4,192,1024]{3,2,1,0:T(8,128)(2,1)} %pick.6.x_ref.xs_ref, ...), custom_call_target="tpu_custom_call", output_to_operand_aliasing={{0}: (6, {}), {1}: (7, {}), {2}: (8, {})} | custom-call | flops 24159191040 | bytes 37748736 | tf_op jit(solution)/shard_map/act_own/pallas_call | solution.py:215
  401.5 10.4 %collective-permute-done.5.refs_1_ = bf16[1024,1024]{1,0:T(8,128)(2,1)} collective-permute-done((bf16[1024,1024]{1,0:T(8,128)(2,1)}, bf16[1024,1024]{1,0:T(8,128)(2,1)}, u32[]{:S(2)}, u32[]{:S(2)}) %collective-permute-start.5) | collective-permute-done | bytes 2097184 | tf_op jit(solution)/shard_map/ppermute | solution.py:384
  414.2 6.6 all_to_all.40
  420.9 3.7 all-to-all-start.3
  424.7 11.2 %pick.8.x_ref.xs_ref = bf16[4,4,192,1024]{3,2,1,0:T(8,128)(2,1)} custom-call(s32[10]{0:T(128)} %stack.43.base_ref._, f32[8,8,1024]{2,1,0:T(8,128)} %bitcast.48, bf16[4,1024,1024]{2,1,0:T(8,128)(2,1)} %bitcast.35), custom_call_target="tpu_custom_call" | custom-call | flops 6442450944 | bytes 16777216 | tf_op jit(solution)/shard_map/pick/pallas_call | solution.py:115
  435.9 7.2 add_back.3.refs_3_
  443.8 12.0 %pick_other.4.x_ref.xo_ref = bf16[4,4,192,1024]{3,2,1,0:T(8,128)(2,1)} custom-call(s32[10]{0:T(128)} %stack.43.base_ref._, f32[8,8,1024]{2,1,0:T(8,128)} %bitcast.49, bf16[1024,1024]{1,0:T(8,128)(2,1)} %collective-permute-done.refs_0_, bf16[1024,1024]{1,0:T(8,128)(2,1)} %collective-permute-done.1.refs_1_, bf16[1024,1024]{1,0:T(8,128)(2,1)} %collective-permute-done.2.refs_2_, ...), custom_call_target="tpu_custom_call" | custom-call | flops 6442450944 | bytes 16777216 | tf_op jit(solution)/shard_map/pick_other/pallas_call | solution.py:115
  455.8 12.8 %pick_other.5 = (bf16[4,4,192,1024]{3,2,1,0:T(8,128)(2,1)}, f32[4,4,192,128]{3,2,1,0:T(8,128)}) custom-call(s32[10]{0:T(128)} %stack.43.base_ref._, f32[8,8,1024]{2,1,0:T(8,128)} %bitcast.50, bf16[1024,1024]{1,0:T(8,128)(2,1)} %collective-permute-done.4.refs_0_, bf16[1024,1024]{1,0:T(8,128)(2,1)} %collective-permute-done.5.refs_1_, ...), custom_call_target="tpu_custom_call" | custom-call | flops 6442450944 | bytes 16777216 | tf_op jit(solution)/shard_map/pick_other/pallas_call | solution.py:115
  470.3 8.2 add_back.4.refs_0_
  480.0 3.1 dynamic-slice_bitcast_fusion.1
  485.1 6.4 gate_back.3
  493.4 43.1 %act_other.2 = (bf16[4,4,192,1536]{3,2,1,0:T(8,128)(2,1)}, bf16[4,4,192,1536]{3,2,1,0:T(8,128)(2,1)}, bf16[4,4,192,1536]{3,2,1,0:T(8,128)(2,1)}) custom-call(bf16[4,4,192,1024]{3,2,1,0:T(8,128)(2,1)} %pick_other.4.x_ref.xo_ref, bf16[4,4,192,1024]{3,2,1,0:T(8,128)(2,1)} %get-tuple-element.127.dy_ref.dyo_ref, ...), custom_call_target="tpu_custom_call" | custom-call | flops 28991029248 | bytes 75497472 | tf_op jit(solution)/shard_map/act_other/pallas_call | solution.py:215
  536.5 5.4 all-to-all-start.5
  541.9 12.0 %pick.9 = (bf16[4,4,192,1024]{3,2,1,0:T(8,128)(2,1)}, f32[4,4,192,128]{3,2,1,0:T(8,128)}) custom-call(s32[10]{0:T(128)} %stack.43.base_ref._, f32[8,8,1024]{2,1,0:T(8,128)} %bitcast.51, bf16[4,1024,1024]{2,1,0:T(8,128)(2,1)} %bitcast.41), custom_call_target="tpu_custom_call" | custom-call | flops 6442450944 | bytes 16777216 | tf_op jit(solution)/shard_map/pick/pallas_call | solution.py:115
  557.5 66.9 %act_own.5 = (bf16[4,4,192,1536]{3,2,1,0:T(8,128)(2,1)}, bf16[4,4,192,1536]{3,2,1,0:T(8,128)(2,1)}, bf16[4,4,192,1536]{3,2,1,0:T(8,128)(2,1)}, bf16[4,4,192,1024]{3,2,1,0:T(8,128)(2,1)}, f32[4,4,192,128]{3,2,1,0:T(8,128)}) custom-call(bf16[4,4,192,1024]{3,2,1,0:T(8,128)(2,1)} %pick.8.x_ref.xs_ref, ...), custom_call_target="tpu_custom_call" | custom-call | flops 48318382080 | bytes 75497472 | tf_op jit(solution)/shard_map/act_own/pallas_call | solution.py:215
  624.4 37.2 %collective-permute-done.13.refs_1_ = bf16[1024,1024]{1,0:T(8,128)(2,1)} collective-permute-done((bf16[1024,1024]{1,0:T(8,128)(2,1)}, bf16[1024,1024]{1,0:T(8,128)(2,1)}, u32[]{:S(2)}, u32[]{:S(2)}) %collective-permute-start.13) | collective-permute-done | bytes 2097184 | tf_op jit(solution)/shard_map/ppermute | solution.py:384
  664.3 3.2 all-to-all-start.7
  668.5 47.7 %dweights.3 = (f32[4,512,1536]{2,1,0:T(8,128)}, f32[4,512,1536]{2,1,0:T(8,128)}, f32[4,768,1024]{2,1,0:T(8,128)}) custom-call(s32[10]{0:T(128)} %stack.43.base_ref._, bf16[4,4,192,1024]{3,2,1,0:T(8,128)(2,1)} %pick.6.x_ref.xs_ref, bf16[4,4,192,1024]{3,2,1,0:T(8,128)(2,1)} %pick_other.4.x_ref.xo_ref, ...), custom_call_target="tpu_custom_call" | custom-call | flops 28991029248 | bytes 84934656 | tf_op jit(solution)/shard_map/dweights/pallas_call | solution.py:254
  716.3 18.1 %mix.5 = bf16[1024,1024]{1,0:T(8,128)(2,1)} custom-call(bf16[1024,1024]{1,0:T(8,128)(2,1)} %mix.4.refs_0_, f32[1024,128]{1,0:T(8,128)} %get-tuple-element.96.refs_0_.refs_1_.plan_ref, bf16[3072,1024]{1,0:T(8,128)(2,1)} %bitcast.22.refs_2_), custom_call_target="tpu_custom_call" | custom-call | flops 12884901888 | bytes 6291456 | tf_op jit(solution)/shard_map/mix/pallas_call | solution.py:324
  734.4 5.5 all-to-all-start.6
  740.5 6.4 gate_back.2
  748.8 12.0 %pick_other.6.x_ref.xo_ref = bf16[4,4,192,1024]{3,2,1,0:T(8,128)(2,1)} custom-call(s32[10]{0:T(128)} %stack.43.base_ref._, f32[8,8,1024]{2,1,0:T(8,128)} %bitcast.52, bf16[1024,1024]{1,0:T(8,128)(2,1)} %collective-permute-done.8.refs_0_, bf16[1024,1024]{1,0:T(8,128)(2,1)} %collective-permute-done.9.refs_1_, ...), custom_call_target="tpu_custom_call" | custom-call | flops 6442450944 | bytes 16777216 | tf_op jit(solution)/shard_map/pick_other/pallas_call | solution.py:115
  762.1 12.8 %pick_other.7 = (bf16[4,4,192,1024]{3,2,1,0:T(8,128)(2,1)}, f32[4,4,192,128]{3,2,1,0:T(8,128)}) custom-call(s32[10]{0:T(128)} %stack.43.base_ref._, f32[8,8,1024]{2,1,0:T(8,128)} %bitcast.53, bf16[1024,1024]{1,0:T(8,128)(2,1)} %collective-permute-done.12.refs_0_, bf16[1024,1024]{1,0:T(8,128)(2,1)} %collective-permute-done.13.refs_1_, ...), custom_call_target="tpu_custom_call" | custom-call | flops 6442450944 | bytes 16777216 | tf_op jit(solution)/shard_map/pick_other/pallas_call | solution.py:115
  774.9 42.9 %act_other.3 = (bf16[4,4,192,1536]{3,2,1,0:T(8,128)(2,1)}, bf16[4,4,192,1536]{3,2,1,0:T(8,128)(2,1)}, bf16[4,4,192,1536]{3,2,1,0:T(8,128)(2,1)}) custom-call(bf16[4,4,192,1024]{3,2,1,0:T(8,128)(2,1)} %pick_other.6.x_ref.xo_ref, bf16[4,4,192,1024]{3,2,1,0:T(8,128)(2,1)} %get-tuple-element.151.dy_ref.dyo_ref, ...), custom_call_target="tpu_custom_call" | custom-call | flops 28991029248 | bytes 75497472 | tf_op jit(solution)/shard_map/act_other/pallas_call | solution.py:215
  817.8 48.1 %dweights.2 = (f32[4,512,1536]{2,1,0:T(8,128)}, f32[4,512,1536]{2,1,0:T(8,128)}, f32[4,768,1024]{2,1,0:T(8,128)}) custom-call(s32[10]{0:T(128)} %stack.43.base_ref._, bf16[4,4,192,1024]{3,2,1,0:T(8,128)(2,1)} %pick.8.x_ref.xs_ref, bf16[4,4,192,1024]{3,2,1,0:T(8,128)(2,1)} %pick_other.6.x_ref.xo_ref, ...), custom_call_target="tpu_custom_call" | custom-call | flops 28991029248 | bytes 84934656 | tf_op jit(solution)/shard_map/dweights/pallas_call | solution.py:254
  865.9 11.5 %add_back.5 = bf16[1024,1024]{1,0:T(8,128)(2,1)} custom-call(bf16[1024,1024]{1,0:T(8,128)(2,1)} %add_back.4.refs_0_, f32[1024,128]{1,0:T(8,128)} %get-tuple-element.96.refs_0_.refs_1_.plan_ref, bf16[3072,1024]{1,0:T(8,128)(2,1)} %bitcast.23.refs_2_), custom_call_target="tpu_custom_call" | custom-call | flops 6442450944 | bytes 6291456 | tf_op jit(solution)/shard_map/add_back/pallas_call | solution.py:324
  (72 shorter events, 32.5 us)
Async XLA Ops:
  7.2 62.2 %all-gather.12.cloned.1.call-start = ((), (), s32[]{:S(2)}) async-start(), calls=%async_computation.8 | async-start | bytes 10485760 | tf_op jit(solution)/shard_map/all_gather | solution.py:380
  101.2 40.6 %all-to-all-start = ((bf16[4,2,192,1024]{3,2,1,0:T(8,128)(2,1)}), bf16[4,2,192,1024]{3,2,1,0:T(8,128)(2,1)S(1)}, u32[]{:S(2)}, u32[]{:S(2)}) async-start(bf16[4,2,192,1024]{3,2,1,0:T(8,128)(2,1)} %ffn.3), calls=%async_computation | async-start | bytes 6291456 | tf_op jit(solution)/shard_map/all_to_all | solution.py:376
  141.7 14.6 %copy-start.3 = (bf16[4,2,192,1024]{3,2,1,0:T(8,128)(2,1)}, bf16[4,2,192,1024]{3,2,1,0:T(8,128)(2,1)S(1)}, u32[]{:S(2)}) copy-start(bf16[4,2,192,1024]{3,2,1,0:T(8,128)(2,1)S(1)} %all-to-all-done) | copy-start | bytes 9437188
  141.7 41.6 %all-to-all-start.1 = ((bf16[4,2,192,1024]{3,2,1,0:T(8,128)(2,1)}), bf16[4,2,192,1024]{3,2,1,0:T(8,128)(2,1)}, u32[]{:S(2)}, u32[]{:S(2)}) async-start(bf16[4,2,192,1024]{3,2,1,0:T(8,128)(2,1)} %ffn.4), calls=%async_computation.1 | async-start | bytes 6291456 | tf_op jit(solution)/shard_map/all_to_all | solution.py:376
  146.4 103.7 %all-gather.14.cloned.1.call-start = ((), (), s32[]{:S(2)}) async-start(), calls=%async_computation.9 | async-start | bytes 10485760 | tf_op jit(solution)/shard_map/all_gather | solution.py:380
  194.4 2.8 copy-start.1
  194.5 112.7 %all-gather.16.cloned.1.call-start = ((), (), s32[]{:S(2)}) async-start(), calls=%async_computation.10 | async-start | bytes 10485760 | tf_op jit(solution)/shard_map/all_gather | solution.py:380
  195.2 229.5 %all-gather.18.cloned.1.call-start = ((), (), s32[]{:S(2)}) async-start(), calls=%async_computation.11 | async-start | bytes 10485760 | tf_op jit(solution)/shard_map/all_gather | solution.py:380
  195.8 169.2 %collective-permute-start = (bf16[1024,1024]{1,0:T(8,128)(2,1)}, bf16[1024,1024]{1,0:T(8,128)(2,1)}, u32[]{:S(2)}, u32[]{:S(2)}) collective-permute-start(bf16[1024,1024]{1,0:T(8,128)(2,1)} %mix.4.refs_0_), channel_id=1, source_target_pairs={{0,4},{4,0},{1,5},{5,1},{2,6},{6,2},{3,7},{7,3}} | collective-permute-start | bytes 6291464 | tf_op jit(solution)/shard_map/ppermute | solution.py:384
  197.2 204.2 %collective-permute-start.4 = (bf16[1024,1024]{1,0:T(8,128)(2,1)S(1)}, bf16[1024,1024]{1,0:T(8,128)(2,1)}, u32[]{:S(2)}, u32[]{:S(2)}) collective-permute-start(bf16[1024,1024]{1,0:T(8,128)(2,1)S(1)} %copy-done.1), channel_id=1, source_target_pairs={{0,4},{4,0},{1,5},{5,1},{2,6},{6,2},{3,7},{7,3}} | collective-permute-start | bytes 6291464 | tf_op jit(solution)/shard_map/ppermute | solution.py:384
  253.1 111.9 %collective-permute-start.1 = (bf16[1024,1024]{1,0:T(8,128)(2,1)}, bf16[1024,1024]{1,0:T(8,128)(2,1)}, u32[]{:S(2)}, u32[]{:S(2)}) collective-permute-start(bf16[1024,1024]{1,0:T(8,128)(2,1)} %dynamic-slice_bitcast_fusion.3), channel_id=1, source_target_pairs={{0,4},{4,0},{1,5},{5,1},{2,6},{6,2},{3,7},{7,3}} | collective-permute-start | bytes 6291464 | tf_op jit(solution)/shard_map/ppermute | solution.py:384
  355.3 46.1 %all-to-all-start.2 = ((bf16[4,2,192,1024]{3,2,1,0:T(8,128)(2,1)}), bf16[4,2,192,1024]{3,2,1,0:T(8,128)(2,1)}, u32[]{:S(2)}, u32[]{:S(2)}) async-start(bf16[4,2,192,1024]{3,2,1,0:T(8,128)(2,1)} %get-tuple-element.104), calls=%async_computation.2 | async-start | bytes 6291456 | tf_op jit(solution)/shard_map/all_to_all | solution.py:376
  363.5 48.3 %collective-permute-start.5 = (bf16[1024,1024]{1,0:T(8,128)(2,1)}, bf16[1024,1024]{1,0:T(8,128)(2,1)}, u32[]{:S(2)}, u32[]{:S(2)}) collective-permute-start(bf16[1024,1024]{1,0:T(8,128)(2,1)} %dynamic-slice_bitcast_fusion.2), channel_id=1, source_target_pairs={{0,4},{4,0},{1,5},{5,1},{2,6},{6,2},{3,7},{7,3}} | collective-permute-start | bytes 6291464 | tf_op jit(solution)/shard_map/ppermute | solution.py:384
  365.0 78.8 %collective-permute-start.2 = (bf16[1024,1024]{1,0:T(8,128)(2,1)}, bf16[1024,1024]{1,0:T(8,128)(2,1)}, u32[]{:S(2)}, u32[]{:S(2)}) collective-permute-start(bf16[1024,1024]{1,0:T(8,128)(2,1)} %collective-permute-done.refs_0_), channel_id=1, source_target_pairs={{0,1},{1,0},{2,3},{3,2},{4,5},{5,4},{6,7},{7,6}} | collective-permute-start | bytes 6291464 | tf_op jit(solution)/shard_map/ppermute | solution.py:388
  365.2 78.6 %collective-permute-start.3 = (bf16[1024,1024]{1,0:T(8,128)(2,1)}, bf16[1024,1024]{1,0:T(8,128)(2,1)}, u32[]{:S(2)}, u32[]{:S(2)}) collective-permute-start(bf16[1024,1024]{1,0:T(8,128)(2,1)} %collective-permute-done.1.refs_1_), channel_id=1, source_target_pairs={{0,1},{1,0},{2,3},{3,2},{4,5},{5,4},{6,7},{7,6}} | collective-permute-start | bytes 6291464 | tf_op jit(solution)/shard_map/ppermute | solution.py:388
  365.5 46.9 %copy-start.4 = (f32[4,2,192,128]{3,2,1,0:T(8,128)S(1)}, f32[4,2,192,128]{3,2,1,0:T(8,128)}, u32[]{:S(2)}) copy-start(f32[4,2,192,128]{3,2,1,0:T(8,128)} %get-tuple-element.114) | copy-start | bytes 2359300
  411.9 43.9 %collective-permute-start.6 = (bf16[1024,1024]{1,0:T(8,128)(2,1)}, bf16[1024,1024]{1,0:T(8,128)(2,1)}, u32[]{:S(2)}, u32[]{:S(2)}) collective-permute-start(bf16[1024,1024]{1,0:T(8,128)(2,1)} %collective-permute-done.4.refs_0_), channel_id=1, source_target_pairs={{0,1},{1,0},{2,3},{3,2},{4,5},{5,4},{6,7},{7,6}} | collective-permute-start | bytes 6291464 | tf_op jit(solution)/shard_map/ppermute | solution.py:388
  411.9 43.9 %collective-permute-start.7 = (bf16[1024,1024]{1,0:T(8,128)(2,1)}, bf16[1024,1024]{1,0:T(8,128)(2,1)}, u32[]{:S(2)}, u32[]{:S(2)}) collective-permute-start(bf16[1024,1024]{1,0:T(8,128)(2,1)} %collective-permute-done.5.refs_1_), channel_id=1, source_target_pairs={{0,1},{1,0},{2,3},{3,2},{4,5},{5,4},{6,7},{7,6}} | collective-permute-start | bytes 6291464 | tf_op jit(solution)/shard_map/ppermute | solution.py:388
  420.9 47.7 %all-to-all-start.3 = ((bf16[4,2,192,1024]{3,2,1,0:T(8,128)(2,1)}), bf16[4,2,192,1024]{3,2,1,0:T(8,128)(2,1)S(1)}, u32[]{:S(2)}, u32[]{:S(2)}) async-start(bf16[4,2,192,1024]{3,2,1,0:T(8,128)(2,1)} %get-tuple-element.113), calls=%async_computation.3 | async-start | bytes 6291456 | tf_op jit(solution)/shard_map/all_to_all | solution.py:376
  424.6 111.9 %all-gather.20.cloned.1.call-start = ((), (), s32[]{:S(2)}) async-start(), calls=%async_computation.12 | async-start | bytes 10485760 | tf_op jit(solution)/shard_map/all_gather | solution.py:380
  468.6 1.7 copy-start
  478.5 5.2 copy-start.2
  478.5 183.1 %collective-permute-start.8 = (bf16[1024,1024]{1,0:T(8,128)(2,1)}, bf16[1024,1024]{1,0:T(8,128)(2,1)}, u32[]{:S(2)}, u32[]{:S(2)}) collective-permute-start(bf16[1024,1024]{1,0:T(8,128)(2,1)} %refs_0_.1), channel_id=1, source_target_pairs={{0,4},{4,0},{1,5},{5,1},{2,6},{6,2},{3,7},{7,3}} | collective-permute-start | bytes 6291464 | tf_op jit(solution)/shard_map/ppermute | solution.py:384
  483.1 178.5 %collective-permute-start.9 = (bf16[1024,1024]{1,0:T(8,128)(2,1)}, bf16[1024,1024]{1,0:T(8,128)(2,1)}, u32[]{:S(2)}, u32[]{:S(2)}) collective-permute-start(bf16[1024,1024]{1,0:T(8,128)(2,1)} %dynamic-slice_bitcast_fusion.1), channel_id=1, source_target_pairs={{0,4},{4,0},{1,5},{5,1},{2,6},{6,2},{3,7},{7,3}} | collective-permute-start | bytes 6291464 | tf_op jit(solution)/shard_map/ppermute | solution.py:384
  483.7 140.6 %collective-permute-start.12 = (bf16[1024,1024]{1,0:T(8,128)(2,1)S(1)}, bf16[1024,1024]{1,0:T(8,128)(2,1)}, u32[]{:S(2)}, u32[]{:S(2)}) collective-permute-start(bf16[1024,1024]{1,0:T(8,128)(2,1)S(1)} %copy-done.2), channel_id=1, source_target_pairs={{0,4},{4,0},{1,5},{5,1},{2,6},{6,2},{3,7},{7,3}} | collective-permute-start | bytes 6291464 | tf_op jit(solution)/shard_map/ppermute | solution.py:384
  536.5 87.9 %all-to-all-start.5 = ((bf16[4,4,192,1024]{3,2,1,0:T(8,128)(2,1)}), bf16[4,4,192,1024]{3,2,1,0:T(8,128)(2,1)}, u32[]{:S(2)}, u32[]{:S(2)}) async-start(bf16[4,4,192,1024]{3,2,1,0:T(8,128)(2,1)} %ffn.5), calls=%async_computation.5 | async-start | bytes 12582912 | tf_op jit(solution)/shard_map/all_to_all | solution.py:376
  557.0 104.6 %collective-permute-start.13 = (bf16[1024,1024]{1,0:T(8,128)(2,1)}, bf16[1024,1024]{1,0:T(8,128)(2,1)}, u32[]{:S(2)}, u32[]{:S(2)}) collective-permute-start(bf16[1024,1024]{1,0:T(8,128)(2,1)} %dynamic-slice_bitcast_fusion), channel_id=1, source_target_pairs={{0,4},{4,0},{1,5},{5,1},{2,6},{6,2},{3,7},{7,3}} | collective-permute-start | bytes 6291464 | tf_op jit(solution)/shard_map/ppermute | solution.py:384
  664.3 70.1 %all-to-all-start.7 = ((f32[4,4,192]{2,1,0:T(4,128)}), f32[4,4,192]{2,1,0:T(4,128)S(1)}, u32[]{:S(2)}, u32[]{:S(2)}) async-start(f32[4,4,192]{2,1,0:T(4,128)} %slice_reduce_fusion), calls=%async_computation.7 | async-start | bytes 32768 | tf_op jit(solution)/shard_map/all_to_all | solution.py:376
  667.5 81.3 %collective-permute-start.10 = (bf16[1024,1024]{1,0:T(8,128)(2,1)}, bf16[1024,1024]{1,0:T(8,128)(2,1)}, u32[]{:S(2)}, u32[]{:S(2)}) collective-permute-start(bf16[1024,1024]{1,0:T(8,128)(2,1)} %collective-permute-done.8.refs_0_), channel_id=1, source_target_pairs={{0,1},{1,0},{2,3},{3,2},{4,5},{5,4},{6,7},{7,6}} | collective-permute-start | bytes 6291464 | tf_op jit(solution)/shard_map/ppermute | solution.py:388
  668.0 80.8 %collective-permute-start.11 = (bf16[1024,1024]{1,0:T(8,128)(2,1)}, bf16[1024,1024]{1,0:T(8,128)(2,1)}, u32[]{:S(2)}, u32[]{:S(2)}) collective-permute-start(bf16[1024,1024]{1,0:T(8,128)(2,1)} %collective-permute-done.9.refs_1_), channel_id=1, source_target_pairs={{0,1},{1,0},{2,3},{3,2},{4,5},{5,4},{6,7},{7,6}} | collective-permute-start | bytes 6291464 | tf_op jit(solution)/shard_map/ppermute | solution.py:388
  668.0 92.7 %collective-permute-start.14 = (bf16[1024,1024]{1,0:T(8,128)(2,1)}, bf16[1024,1024]{1,0:T(8,128)(2,1)S(1)}, u32[]{:S(2)}, u32[]{:S(2)}) collective-permute-start(bf16[1024,1024]{1,0:T(8,128)(2,1)} %collective-permute-done.12.refs_0_), channel_id=1, source_target_pairs={{0,1},{1,0},{2,3},{3,2},{4,5},{5,4},{6,7},{7,6}} | collective-permute-start | bytes 6291464 | tf_op jit(solution)/shard_map/ppermute | solution.py:388
  668.5 92.3 %collective-permute-start.15 = (bf16[1024,1024]{1,0:T(8,128)(2,1)}, bf16[1024,1024]{1,0:T(8,128)(2,1)}, u32[]{:S(2)}, u32[]{:S(2)}) collective-permute-start(bf16[1024,1024]{1,0:T(8,128)(2,1)} %collective-permute-done.13.refs_1_), channel_id=1, source_target_pairs={{0,1},{1,0},{2,3},{3,2},{4,5},{5,4},{6,7},{7,6}} | collective-permute-start | bytes 6291464 | tf_op jit(solution)/shard_map/ppermute | solution.py:388
  734.4 131.5 %all-to-all-start.6 = ((bf16[4,4,192,1024]{3,2,1,0:T(8,128)(2,1)}), bf16[4,4,192,1024]{3,2,1,0:T(8,128)(2,1)}, u32[]{:S(2)}, u32[]{:S(2)}) async-start(bf16[4,4,192,1024]{3,2,1,0:T(8,128)(2,1)} %get-tuple-element.145), calls=%async_computation.6 | async-start | bytes 12582912 | tf_op jit(solution)/shard_map/all_to_all | solution.py:376
  760.8 1.3 copy-start.5
Sparse Core Ops, SparseCore 0:
  9.5 59.8 all-gather.11
  194.6 55.4 all-gather.13
  251.6 55.4 all-gather.15
  308.5 55.4 all-gather.17
  478.7 56.8 all-gather.19
